TPU v7x, 32 devices: a whole 2x2x4 slice. The times are simulated.
32 devices in a mesh: fsdp: 4 (over x, core), ctx: 4 (over z), tp: 2 (over y).
Axes of the slice: x: 2, y: 2, z: 4, core: 2. Of those that a mesh axis runs over, the one named last changes fastest.
Arguments:
- tokens: bfloat16 [8192, 2048], P(('fsdp', 'ctx')), may hold values from -6 to 6
- cotangent: bfloat16 [8192, 2048], P(('fsdp', 'ctx')), may hold values from -6 to 6
- sequence_begin: int32 [8192], P('fsdp'), may hold values from 0 to 2047, as said below
- piece: int32 [8192], P('fsdp'), may hold values from 0 to 8, as said below
- padding_length: int32 [4], P('fsdp'), may hold values from 0 to 256, as said below
- attn_gain: bfloat16 [2048], P(('fsdp', 'ctx')), may hold values from 0.5 to 1.5
- q_gain: bfloat16 [128], P(('fsdp', 'ctx')), may hold values from 0.5 to 2
- k_gain: bfloat16 [128], P(('fsdp', 'ctx')), may hold values from 0.5 to 2
- w_query: bfloat16 [2048, 2048], P(('fsdp', 'ctx'), 'tp'), may hold values from -0.125 to 0.125
- key_weight: bfloat16 [2048, 1024], P(('fsdp', 'ctx'), 'tp'), may hold values from -0.125 to 0.125
- value_weight: bfloat16 [2048, 1024], P(('fsdp', 'ctx'), 'tp'), may hold values from -0.125 to 0.125
- w_out: bfloat16 [2048, 2048], P(('fsdp', 'ctx'), 'tp'), may hold values from -1 to 1
- mlp_gain: bfloat16 [2048], P(('fsdp', 'ctx')), may hold values from 0.5 to 1.5
- w_gate: bfloat16 [2048, 6144], P(('fsdp', 'ctx'), 'tp'), may hold values from -0.125 to 0.125
- w_up: bfloat16 [2048, 6144], P(('fsdp', 'ctx'), 'tp'), may hold values from -0.125 to 0.125
- w_down: bfloat16 [2048, 6144], P(('fsdp', 'ctx'), 'tp'), may hold values from -0.078125 to 0.078125
Outputs:
- layer_out: bfloat16 [8192, 2048], P(('fsdp', 'ctx'))
- grad_tokens: bfloat16 [8192, 2048], P(('fsdp', 'ctx'))
- grad_attn_gain: float32 [2048], P(('fsdp', 'ctx'))
- grad_q_gain: float32 [128], P(('fsdp', 'ctx'))
- grad_k_gain: float32 [128], P(('fsdp', 'ctx'))
- grad_query: float32 [2048, 2048], P(('fsdp', 'ctx'), 'tp')
- grad_key: float32 [2048, 1024], P(('fsdp', 'ctx'), 'tp')
- grad_value: float32 [2048, 1024], P(('fsdp', 'ctx'), 'tp')
- grad_out: float32 [2048, 2048], P(('fsdp', 'ctx'), 'tp')
- grad_mlp_gain: float32 [2048], P(('fsdp', 'ctx'))
- grad_gate: float32 [2048, 6144], P(('fsdp', 'ctx'), 'tp')
- grad_up: float32 [2048, 6144], P(('fsdp', 'ctx'), 'tp')
- grad_down: float32 [2048, 6144], P(('fsdp', 'ctx'), 'tp')
Inputs may be any that keep to these rules, and one draw needn't show every extreme that they name: `sequence_begin`: each group of 2048 tokens holds a first sequence of 1024 or more tokens from index 0, perhaps a second one after it, then its padding tokens, which form a sequence of their own; entries are indices within the group. The 256 tokens of one aligned block of 256 positions inside one sequence may form a picture piece and then share a positive number unique in the group; all other tokens are 0. `padding_length`: some group has exactly 256 padding tokens.
All inputs are finite; a program needn't handle non-finite values.
Results may differ from a plain program's by a relative error of at most 0.02.
Values may be sent and summed in bfloat16 or wider, within the bound.
A program may use at most 256 MiB of HBM per device.

v0:
```python
import jax
import jax.numpy as jnp
from jax import lax
from jax.sharding import PartitionSpec as P

HEAD_SIZE = 128


EPS = 1e-06
THETA = 1000000.0
MASK_FILL = -1e30


def rms_scale(features, gain_vec):
    inverse = lax.rsqrt(jnp.mean(features * features, axis=-1, keepdims=True) + EPS)
    return features * inverse * gain_vec


def rotate(features, cosine, sine):
    half_width = features.shape[-1] // 2
    turned = jnp.concatenate([-features[..., half_width:], features[..., :half_width]], axis=-1)
    return features * cosine + turned * sine


def rope_tables(positions, width):
    half_width = width // 2
    frequency = THETA ** (-(jnp.arange(half_width, dtype=jnp.float32) * 2.0 / width))
    angles = positions[:, None] * frequency[None, :]
    angles = jnp.concatenate([angles, angles], axis=-1)
    return (jnp.cos(angles)[:, None, :], jnp.sin(angles)[:, None, :])


def allowed(query_index, key_index, start_query, start_key, piece_query, piece_key, key_live):
    same_doc = start_query[:, None] == start_key[None, :]
    causal_pair = key_index[None, :] <= query_index[:, None]
    picture_pair = (piece_query[:, None] == piece_key[None, :]) & (piece_query[:, None] > 0)
    live_key = key_live[None, :] | (key_index[None, :] == query_index[:, None])
    return same_doc & (causal_pair | picture_pair) & live_key


def contract_last(left_side, right_side):
    return lax.dot_general(
        left_side, right_side, (((1,), (1,)), ((), ())), preferred_element_type=jnp.float32
    )


def contract_first(left_side, right_side):
    return lax.dot_general(
        left_side, right_side, (((0,), (0,)), ((), ())), preferred_element_type=jnp.float32
    )


def body(
    tokens,
    cotangent,
    sequence_begin,
    piece,
    padding_length,
    attn_gain,
    q_gain,
    k_gain,
    w_query,
    key_weight,
    value_weight,
    w_out,
    mlp_gain,
    w_gate,
    w_up,
    w_down,
):
    f32 = jnp.float32
    bf16 = jnp.bfloat16
    tok_rows = tokens.shape[0]
    group_rows = sequence_begin.shape[0]
    offset = lax.axis_index("ctx") * tok_rows
    local_index = offset + jnp.arange(tok_rows, dtype=jnp.int32)
    my_start = lax.dynamic_slice_in_dim(sequence_begin, offset, tok_rows)
    cosine, sine = rope_tables((local_index - my_start).astype(f32), HEAD_SIZE)
    key_index = jnp.arange(group_rows, dtype=jnp.int32)
    key_live = key_index < group_rows - padding_length[0]
    score_scale = HEAD_SIZE ** (-0.5)
    block_rows = min(512, group_rows)
    starts = jnp.arange(group_rows // block_rows, dtype=jnp.int32) * block_rows

    def head_prep(raw_heads, gain_vec):
        return rotate(rms_scale(raw_heads, gain_vec), cosine, sine)

    g_attn, g_query, g_key, wq_full, key_weight_whole, value_weight_whole, wo_full = (
        lax.all_gather(attn_gain, ("fsdp", "ctx"), axis=0, tiled=True),
        lax.all_gather(q_gain, ("fsdp", "ctx"), axis=0, tiled=True),
        lax.all_gather(k_gain, ("fsdp", "ctx"), axis=0, tiled=True),
        lax.all_gather(w_query, ("fsdp", "ctx"), axis=0, tiled=True),
        lax.all_gather(key_weight, ("fsdp", "ctx"), axis=0, tiled=True),
        lax.all_gather(value_weight, ("fsdp", "ctx"), axis=0, tiled=True),
        lax.all_gather(w_out, ("fsdp", "ctx"), axis=0, tiled=True),
    )
    attn_gain_f = g_attn.astype(f32)
    qgain_f = g_query.astype(f32)
    kgain_f = g_key.astype(f32)
    x_rows = tokens.astype(f32)
    normed_bf = rms_scale(x_rows, attn_gain_f).astype(bf16)
    q_raw = jnp.dot(normed_bf, wq_full, preferred_element_type=f32).reshape(tok_rows, -1, HEAD_SIZE)
    key_unrotated = jnp.dot(normed_bf, key_weight_whole, preferred_element_type=f32).reshape(
        tok_rows, -1, HEAD_SIZE
    )
    v_tok = (
        jnp.dot(normed_bf, value_weight_whole, preferred_element_type=f32)
        .astype(bf16)
        .reshape(tok_rows, -1, HEAD_SIZE)
    )
    q_tok = head_prep(q_raw, qgain_f).astype(bf16)
    k_tok = head_prep(key_unrotated, kgain_f).astype(bf16)
    q_head, k_head, v_head = (
        lax.all_to_all(q_tok, "ctx", split_axis=1, concat_axis=0, tiled=True),
        lax.all_to_all(k_tok, "ctx", split_axis=1, concat_axis=0, tiled=True),
        lax.all_to_all(v_tok, "ctx", split_axis=1, concat_axis=0, tiled=True),
    )
    kv_heads = k_head.shape[1]
    per_group = q_head.shape[1] // kv_heads
    q_group = q_head.reshape(group_rows, kv_heads, per_group, HEAD_SIZE)

    def block_scores(block_start):
        q_block = lax.dynamic_slice_in_dim(q_group, block_start, block_rows, 0)
        query_index = block_start + jnp.arange(block_rows, dtype=jnp.int32)
        pairs = allowed(
            query_index,
            key_index,
            lax.dynamic_slice_in_dim(sequence_begin, block_start, block_rows),
            sequence_begin,
            lax.dynamic_slice_in_dim(piece, block_start, block_rows),
            piece,
            key_live,
        )
        raw_scores = (
            jnp.einsum("qkrd,skd->qkrs", q_block, k_head, preferred_element_type=f32) * score_scale
        )
        return (q_block, jnp.where(pairs[:, None, None, :], raw_scores, MASK_FILL))

    def forward_block(block_start):
        q_block, scores = block_scores(block_start)
        row_max = jnp.max(scores, axis=-1, keepdims=True)
        expo_scores = jnp.exp(scores - row_max)
        row_total = jnp.sum(expo_scores, axis=-1, keepdims=True)
        prob_rows = (expo_scores / row_total).astype(bf16)
        head_out = jnp.einsum("qkrs,skd->qkrd", prob_rows, v_head, preferred_element_type=f32)
        return (
            head_out.astype(bf16).reshape(block_rows, kv_heads * per_group, HEAD_SIZE),
            (row_max + jnp.log(row_total))[..., 0],
        )

    out_blocks, lse_blocks = lax.map(forward_block, starts)
    o_head = out_blocks.reshape(group_rows, kv_heads * per_group, HEAD_SIZE)
    log_totals = lse_blocks.reshape(group_rows, kv_heads, per_group)
    o_tok = lax.all_to_all(o_head, "ctx", split_axis=0, concat_axis=1, tiled=True).reshape(
        tok_rows, -1
    )
    residual = x_rows + lax.psum(contract_last(o_tok, wo_full), "tp")
    g_mlp, wg_full, wu_full, wd_full = (
        lax.all_gather(mlp_gain, ("fsdp", "ctx"), axis=0, tiled=True),
        lax.all_gather(w_gate, ("fsdp", "ctx"), axis=0, tiled=True),
        lax.all_gather(w_up, ("fsdp", "ctx"), axis=0, tiled=True),
        lax.all_gather(w_down, ("fsdp", "ctx"), axis=0, tiled=True),
    )
    mlp_gain_f = g_mlp.astype(f32)
    normed_two = rms_scale(residual, mlp_gain_f).astype(bf16)
    gate_value = jnp.dot(normed_two, wg_full, preferred_element_type=f32)
    up_value = jnp.dot(normed_two, wu_full, preferred_element_type=f32)
    gate_sigmoid = jax.nn.sigmoid(gate_value)
    gate_silu = gate_value * gate_sigmoid
    hidden = (gate_silu * up_value).astype(bf16)
    layer_out = (
        residual
        + lax.psum(contract_last(hidden, wd_full).astype(jnp.bfloat16), "tp").astype(jnp.float32)
    ).astype(bf16)
    d_hidden = jnp.dot(cotangent, wd_full, preferred_element_type=f32)
    d_gate = (
        d_hidden * up_value * gate_sigmoid * (1.0 + gate_value * (1.0 - gate_sigmoid))
    ).astype(bf16)
    d_up = (d_hidden * gate_silu).astype(bf16)
    d_norm_two = lax.psum(contract_last(d_gate, wg_full) + contract_last(d_up, wu_full), "tp")
    _, pull_two = jax.vjp(rms_scale, residual, mlp_gain_f)
    d_residual, d_mlp_gain = pull_two(d_norm_two)
    d_residual = d_residual + cotangent.astype(f32)
    d_branch = d_residual.astype(bf16)
    d_out = (
        jnp.dot(d_branch, wo_full, preferred_element_type=f32)
        .astype(bf16)
        .reshape(tok_rows, -1, HEAD_SIZE)
    )
    d_head = lax.all_to_all(d_out, "ctx", split_axis=1, concat_axis=0, tiled=True).reshape(
        group_rows, kv_heads, per_group, HEAD_SIZE
    )

    def backward_block(accum_pair, block_start):
        key_accum, value_accum = accum_pair
        q_block, scores = block_scores(block_start)
        d_block = lax.dynamic_slice_in_dim(d_head, block_start, block_rows, 0)
        lse_block = lax.dynamic_slice_in_dim(log_totals, block_start, block_rows, 0)
        prob_rows = jnp.exp(scores - lse_block[..., None])
        d_probs = jnp.einsum("qkrd,skd->qkrs", d_block, v_head, preferred_element_type=f32)
        delta_rows = jnp.sum(prob_rows * d_probs, axis=-1, keepdims=True)
        d_scores = (prob_rows * (d_probs - delta_rows)).astype(bf16)
        d_query = (
            jnp.einsum("qkrs,skd->qkrd", d_scores, k_head, preferred_element_type=f32) * score_scale
        )
        key_accum = (
            key_accum
            + jnp.einsum("qkrs,qkrd->skd", d_scores, q_block, preferred_element_type=f32)
            * score_scale
        )
        value_accum = value_accum + jnp.einsum(
            "qkrs,qkrd->skd", prob_rows.astype(bf16), d_block, preferred_element_type=f32
        )
        return (
            (key_accum, value_accum),
            d_query.astype(bf16).reshape(block_rows, kv_heads * per_group, HEAD_SIZE),
        )

    zero_state = jnp.zeros((group_rows, kv_heads, HEAD_SIZE), f32)
    (key_accum, value_accum), dq_blocks = lax.scan(backward_block, (zero_state, zero_state), starts)
    dq_head = dq_blocks.reshape(group_rows, kv_heads * per_group, HEAD_SIZE)
    dq_tok, dk_tok, dv_tok = (
        lax.all_to_all(dq_head, "ctx", split_axis=0, concat_axis=1, tiled=True),
        lax.all_to_all(key_accum.astype(bf16), "ctx", split_axis=0, concat_axis=1, tiled=True),
        lax.all_to_all(value_accum.astype(bf16), "ctx", split_axis=0, concat_axis=1, tiled=True),
    )
    _, pull_query = jax.vjp(head_prep, q_raw, qgain_f)
    dq_raw, d_qgain = pull_query(dq_tok.astype(f32))
    _, pull_key = jax.vjp(head_prep, key_unrotated, kgain_f)
    dk_raw, d_kgain = pull_key(dk_tok.astype(f32))
    dq_flat = dq_raw.astype(bf16).reshape(tok_rows, -1)
    dk_flat = dk_raw.astype(bf16).reshape(tok_rows, -1)
    dv_flat = dv_tok.reshape(tok_rows, -1)
    d_norm_part = (
        contract_last(dq_flat, wq_full)
        + contract_last(dk_flat, key_weight_whole)
        + contract_last(dv_flat, value_weight_whole)
    )
    d_norm, d_qgain, d_kgain = lax.psum((d_norm_part, d_qgain, d_kgain), "tp")
    _, pull_one = jax.vjp(rms_scale, x_rows, attn_gain_f)
    d_tokens, d_attn_gain = pull_one(d_norm)
    grad_tokens = (d_residual + d_tokens).astype(bf16)
    all_grads = (
        lax.psum_scatter(d_attn_gain, ("fsdp", "ctx"), scatter_dimension=0, tiled=True),
        lax.psum_scatter(d_qgain, ("fsdp", "ctx"), scatter_dimension=0, tiled=True),
        lax.psum_scatter(d_kgain, ("fsdp", "ctx"), scatter_dimension=0, tiled=True),
        lax.psum_scatter(
            contract_first(normed_bf, dq_flat), ("fsdp", "ctx"), scatter_dimension=0, tiled=True
        ),
        lax.psum_scatter(
            contract_first(normed_bf, dk_flat), ("fsdp", "ctx"), scatter_dimension=0, tiled=True
        ),
        lax.psum_scatter(
            contract_first(normed_bf, dv_flat), ("fsdp", "ctx"), scatter_dimension=0, tiled=True
        ),
        lax.psum_scatter(
            contract_first(d_branch, o_tok), ("fsdp", "ctx"), scatter_dimension=0, tiled=True
        ),
        lax.psum_scatter(d_mlp_gain, ("fsdp", "ctx"), scatter_dimension=0, tiled=True),
        lax.psum_scatter(
            contract_first(normed_two, d_gate), ("fsdp", "ctx"), scatter_dimension=0, tiled=True
        ),
        lax.psum_scatter(
            contract_first(normed_two, d_up), ("fsdp", "ctx"), scatter_dimension=0, tiled=True
        ),
        lax.psum_scatter(
            contract_first(cotangent, hidden), ("fsdp", "ctx"), scatter_dimension=0, tiled=True
        ),
    )
    return (
        layer_out,
        grad_tokens,
        all_grads[0],
        all_grads[1],
        all_grads[2],
        all_grads[3],
        all_grads[4],
        all_grads[5],
        all_grads[6],
        all_grads[7],
        all_grads[8],
        all_grads[9],
        all_grads[10],
    )


def solution(mesh):
    in_specs = (
        P(("fsdp", "ctx"), None),
        P(("fsdp", "ctx"), None),
        P("fsdp"),
        P("fsdp"),
        P("fsdp"),
        P(("fsdp", "ctx")),
        P(("fsdp", "ctx")),
        P(("fsdp", "ctx")),
        P(("fsdp", "ctx"), "tp"),
        P(("fsdp", "ctx"), "tp"),
        P(("fsdp", "ctx"), "tp"),
        P(("fsdp", "ctx"), "tp"),
        P(("fsdp", "ctx")),
        P(("fsdp", "ctx"), "tp"),
        P(("fsdp", "ctx"), "tp"),
        P(("fsdp", "ctx"), "tp"),
    )
    out_specs = (
        P(("fsdp", "ctx"), None),
        P(("fsdp", "ctx"), None),
        P(("fsdp", "ctx")),
        P(("fsdp", "ctx")),
        P(("fsdp", "ctx")),
        P(("fsdp", "ctx"), "tp"),
        P(("fsdp", "ctx"), "tp"),
        P(("fsdp", "ctx"), "tp"),
        P(("fsdp", "ctx"), "tp"),
        P(("fsdp", "ctx")),
        P(("fsdp", "ctx"), "tp"),
        P(("fsdp", "ctx"), "tp"),
        P(("fsdp", "ctx"), "tp"),
    )
    return jax.shard_map(body, mesh=mesh, in_specs=in_specs, out_specs=out_specs, check_vma=False)
```

profile of v0, /device:TPU:0, one launch (start us, length us, event | category | flops | bytes accessed | tf_op | source)
XLA Modules:
  0.0 2411.8 jit_solution(119953250545401077)
XLA Ops:
  9.4 34.1 %all-gather = bf16[16,1,128]{2,1,0:T(2,128)(2,1)S(1)} all-gather(bf16[1,1,128]{2,1,0:T(2,128)(2,1)} %bitcast.402), channel_id=1, replica_groups=mesh['fsdp'=4,'ctx'=4,'tp'=2] {'fsdp','ctx'}, dimensions={0}, use_global_device_ids=true | all-gather | bytes 4352 | tf_op jit(solution)/shard_map/all_gather | solution.py:89
  47.2 29.8 %all-reduce.12 = (bf16[128]{0:T(256)(128)(2,1)S(1)}, bf16[128]{0:T(256)(128)(2,1)S(1)}) all-reduce(bf16[128]{0:T(256)(128)(2,1)S(1)} %dynamic-update-slice, bf16[128]{0:T(256)(128)(2,1)S(1)} %dynamic-update-slice.1), channel_id=1, replica_groups=mesh['fsdp'=4,'ctx'=4,'tp'=2] {'fsdp','ctx'}, use_global_device_ids=true, to_apply=%add.4 | all-reduce | flops 256 | bytes 1024
  102.5 46.5 %all-gather.10.cloned.1.call-done = bf16[2048,1024]{1,0:T(8,128)(2,1)} async-done(((bf16[128,1024]{1,0:T(8,128)(2,1)}), bf16[2048,1024]{1,0:T(8,128)(2,1)}) %all-gather.10.cloned.1.call-update) | async-done | bytes 4194320 | tf_op jit(solution)/shard_map/all_gather | solution.py:92
  183.1 30.7 %all-to-all-done = bf16[512,8,128]{2,0,1:T(8,128)(2,1)} async-done(((bf16[512,8,128]{2,0,1:T(8,128)(2,1)}), bf16[512,8,128]{2,0,1:T(8,128)(2,1)}, u32[]{:S(2)}, u32[]{:S(2)}) %all-to-all-start) | async-done | bytes 1048608 | tf_op jit(solution)/shard_map/all_to_all | solution.py:114
  217.2 61.6 %while.30 = (s32[]{:T(128)}, bf16[4,512,2,128]{3,1,0,2:T(8,128)(2,1)}, f32[4,512,1,2]{1,3,2,0:T(2,128)S(1)}, s32[4]{0:T(128)S(1)}, s32[2048]{0:T(1024)S(1)}, /*i...) while((s32[]{:T(128)}, ...), condition=%wide.region_6.7_spmd.clone.clone, body=%wide.region_3.6_spmd.clone.clone.sunk | while | flops 1108477952 | bytes 31004356 | solution.py:151
  281.6 27.7 %all_to_all.114 = bf16[2048,2,128]{2,1,0:T(2,128)(2,1)S(1)} all-to-all(bf16[2048,2,128]{2,1,0:T(2,128)(2,1)S(1)} %copy.185), channel_id=1, replica_groups=mesh['fsdp'=4,'ctx'=4,'tp'=2] {'ctx'}, dimensions={0} | all-to-all | bytes 2097152 | tf_op jit(solution)/shard_map/all_to_all | solution.py:154
  321.7 28.9 %all-gather.1 = bf16[16,1,128]{2,1,0:T(2,128)(2,1)S(1)} all-gather(bf16[1,1,128]{2,1,0:T(2,128)(2,1)S(1)} %bitcast.403), channel_id=1, replica_groups=mesh['fsdp'=4,'ctx'=4,'tp'=2] {'fsdp','ctx'}, dimensions={0}, use_global_device_ids=true | all-gather | bytes 4352 | tf_op jit(solution)/shard_map/all_gather | solution.py:159
  350.7 75.1 %all-reduce.18.cloned.1.call-done = f32[512,2048]{1,0:T(8,128)} async-done(((f32[512,2048]{1,0:T(8,128)}), f32[512,2048]{1,0:T(8,128)}) %all-reduce.18.cloned.1.call-update) | async-done | bytes 4194320 | tf_op jit(solution)/shard_map/psum | solution.py:157
  431.0 97.4 %all-gather.18.cloned.1.call-done = bf16[2048,3072]{1,0:T(8,128)(2,1)} async-done(((bf16[128,3072]{1,0:T(8,128)(2,1)}), bf16[2048,3072]{1,0:T(8,128)(2,1)}) %all-gather.18.cloned.1.call-update) | async-done | bytes 12582928 | tf_op jit(solution)/shard_map/all_gather | solution.py:160
  539.7 89.7 %all-gather.20.cloned.1.call-done = bf16[2048,3072]{1,0:T(8,128)(2,1)} async-done(((bf16[128,3072]{1,0:T(8,128)(2,1)}), bf16[2048,3072]{1,0:T(8,128)(2,1)}) %all-gather.20.cloned.1.call-update) | async-done | bytes 12582928 | tf_op jit(solution)/shard_map/all_gather | solution.py:161
  629.4 12.0 fusion.129
  641.4 89.0 %all-gather.22.cloned.1.call-done = bf16[2048,3072]{1,0:T(8,128)(2,1)} async-done(((bf16[128,3072]{1,0:T(8,128)(2,1)}), bf16[2048,3072]{1,0:T(8,128)(2,1)}) %all-gather.22.cloned.1.call-update) | async-done | bytes 12582928 | tf_op jit(solution)/shard_map/all_gather | solution.py:162
  730.4 16.4 multiply_convert_fusion
  746.8 13.4 fusion.130
  760.2 12.0 convolution_add_fusion
  783.9 94.6 %all-reduce.22.cloned.1.call-done = f32[512,2048]{1,0:T(8,128)} async-done(((f32[512,2048]{1,0:T(8,128)}), f32[512,2048]{1,0:T(8,128)}) %all-reduce.22.cloned.1.call-update) | async-done | bytes 4194320 | tf_op jit(solution)/shard_map/psum | solution.py:180
  883.7 60.6 %all-reduce.20.cloned.1.call-done = bf16[512,2048]{1,0:T(8,128)(2,1)} async-done(((bf16[512,2048]{1,0:T(8,128)(2,1)}), bf16[512,2048]{1,0:T(8,128)(2,1)}) %all-reduce.20.cloned.1.call-update) | async-done | bytes 2097168 | tf_op jit(solution)/shard_map/psum | solution.py:173
  958.9 25.5 %all-to-all-done.4 = bf16[512,8,128]{2,0,1:T(8,128)(2,1)S(1)} async-done(((bf16[512,8,128]{2,0,1:T(8,128)(2,1)}), bf16[512,8,128]{2,0,1:T(8,128)(2,1)S(1)}, u32[]{:S(2)}, u32[]{:S(2)}) %all-to-all-start.4) | async-done | bytes 1048608 | tf_op jit(solution)/shard_map/all_to_all | solution.py:190
  986.6 117.5 %while.31 = (s32[]{:T(128)}, f32[2048,1,128]{0,2,1:T(8,128)S(1)}, f32[2048,1,128]{0,2,1:T(8,128)}, bf16[4,512,2,128]{3,1,0,2:T(8,128)(2,1)}, s32[4]{0:T(128)S(1)...) while((s32[]{:T(128)}, f32[2048,1,128]{0,2,1:T(8,128)S(1)}, ...), condition=%wide.region_14.15_spmd.clone.clone, body=%wide.region_12.14_spmd.clone.clone.sunk | while | flops 2726823936 | bytes 141362992 | solution.py:220
  1159.8 12.6 all-to-all-done.5
  1190.3 14.3 convolution_bitcast_fusion.1
  1229.6 14.3 fusion.133
  1244.0 14.2 fusion.134
  1258.9 36.0 %all-reduce.24.cloned.1.call-done = f32[512,2048]{1,0:T(8,128)} async-done(((f32[512,2048]{1,0:T(8,128)}), f32[512,2048]{1,0:T(8,128)}) %all-reduce.24.cloned.1.call-update) | async-done | bytes 4194320 | tf_op jit(solution)/shard_map/psum | solution.py:239
  1298.5 62.7 %all-reduce.10 = (f32[2048]{0:T(1024)S(1)}, f32[128]{0:T(128)S(1)}, f32[128]{0:T(128)S(1)}, f32[2048]{0:T(1024)S(1)}) all-reduce(f32[2048]{0:T(1024)S(1)} %get-tuple-element.391, f32[128]{0:T(128)S(1)} %get-tuple-element.393, f32[128]{0:T(128)S(1)} %get-tuple-element.395, ...), channel_id=2, replica_groups=mesh['fsdp'=4,'ctx'=4,'tp'=2] {'fsdp','ctx'}, use_global_device_ids=true, to_apply=%region_20.21.clone | all-reduce | flops 4352 | bytes 34816
  1374.6 167.9 %reduce-scatter.20.cloned.1.call-done = f32[128,3072]{0,1:T(8,128)} async-done(((f32[2048,3072]{0,1:T(8,128)}), f32[128,3072]{0,1:T(8,128)}) %reduce-scatter.20.cloned.1.call-update) | async-done | bytes 1572880 | tf_op jit(solution)/shard_map/reduce_scatter | solution.py:266
  1545.5 73.3 %reduce-scatter.10.cloned.1.call-done = f32[128,512]{1,0:T(8,128)} async-done(((f32[2048,512]{1,0:T(8,128)}), f32[128,512]{1,0:T(8,128)}) %reduce-scatter.10.cloned.1.call-update) | async-done | bytes 262160 | tf_op jit(solution)/shard_map/reduce_scatter | solution.py:250
  1618.8 76.1 %reduce-scatter.12.cloned.1.call-done = f32[128,512]{1,0:T(8,128)} async-done(((f32[2048,512]{1,0:T(8,128)}), f32[128,512]{1,0:T(8,128)}) %reduce-scatter.12.cloned.1.call-update) | async-done | bytes 262160 | tf_op jit(solution)/shard_map/reduce_scatter | solution.py:253
  1694.9 107.0 %reduce-scatter.14.cloned.1.call-done = f32[128,1024]{1,0:T(8,128)} async-done(((f32[2048,1024]{1,0:T(8,128)}), f32[128,1024]{1,0:T(8,128)}) %reduce-scatter.14.cloned.1.call-update) | async-done | bytes 524304 | tf_op jit(solution)/shard_map/reduce_scatter | solution.py:256
  1802.0 107.6 %reduce-scatter.8.cloned.1.call-done = f32[128,1024]{1,0:T(8,128)} async-done(((f32[2048,1024]{1,0:T(8,128)}), f32[128,1024]{1,0:T(8,128)}) %reduce-scatter.8.cloned.1.call-update) | async-done | bytes 524304 | tf_op jit(solution)/shard_map/reduce_scatter | solution.py:247
  1909.6 247.8 %reduce-scatter.16.cloned.1.call-done = f32[128,3072]{1,0:T(8,128)} async-done(((f32[2048,3072]{1,0:T(8,128)}), f32[128,3072]{1,0:T(8,128)}) %reduce-scatter.16.cloned.1.call-update) | async-done | bytes 1572880 | tf_op jit(solution)/shard_map/reduce_scatter | solution.py:260
  2157.3 247.2 %reduce-scatter.18.cloned.1.call-done = f32[128,3072]{1,0:T(8,128)} async-done(((f32[2048,3072]{1,0:T(8,128)}), f32[128,3072]{1,0:T(8,128)}) %reduce-scatter.18.cloned.1.call-update) | async-done | bytes 1572880 | tf_op jit(solution)/shard_map/reduce_scatter | solution.py:263
  (359 shorter events, 413.1 us)
Async XLA Ops:
  7.2 75.3 %all-gather.12.cloned.1.call-start = ((), (), s32[]{:S(2)}) async-start(), calls=%async_computation.16 | async-start | bytes 2228224 | tf_op jit(solution)/shard_map/all_gather | solution.py:93
  7.9 90.8 %all-gather.14.cloned.1.call-start = ((), (), s32[]{:S(2)}) async-start(), calls=%async_computation.17 | async-start | bytes 2228224 | tf_op jit(solution)/shard_map/all_gather | solution.py:94
  8.7 140.3 %all-gather.10.cloned.1.call-start = ((), (), s32[]{:S(2)}) async-start(), calls=%async_computation.15 | async-start | bytes 4456448 | tf_op jit(solution)/shard_map/all_gather | solution.py:92
  43.5 105.5 %copy-start.29 = (f32[16,1,128]{2,1,0:T(1,128)}, f32[16,1,128]{2,1,0:T(1,128)S(1)}, u32[]{:S(2)}) copy-start(f32[16,1,128]{2,1,0:T(1,128)S(1)} %convert_element_type.182) | copy-start | bytes 24580
  77.1 85.9 %copy-start.44 = (f32[128]{0:T(128)}, f32[128]{0:T(128)S(1)}, u32[]{:S(2)}) copy-start(f32[128]{0:T(128)S(1)} %convert_element_type.135) | copy-start | bytes 1540
  79.1 83.8 %copy-start.12 = (f32[512,128]{1,0:T(8,128)}, f32[512,128]{1,0:T(8,128)S(1)}, u32[]{:S(2)}) copy-start(f32[512,128]{1,0:T(8,128)S(1)} %get-tuple-element.476) | copy-start | bytes 786436
  79.1 83.8 %copy-start.14 = (f32[512,128]{1,0:T(8,128)}, f32[512,128]{1,0:T(8,128)S(1)}, u32[]{:S(2)}) copy-start(f32[512,128]{1,0:T(8,128)S(1)} %get-tuple-element.477) | copy-start | bytes 786436
  87.7 68.4 %all-to-all-start.1 = ((bf16[512,4,128]{0,2,1:T(8,128)(2,1)}), bf16[512,4,128]{0,2,1:T(8,128)(2,1)S(1)}, u32[]{:S(2)}, u32[]{:S(2)}) async-start(bf16[512,4,128]{0,2,1:T(8,128)(2,1)} %fusion.99), calls=%async_computation.1 | async-start | bytes 1048576 | tf_op jit(solution)/shard_map/all_to_all | solution.py:115
  156.1 19.4 all-to-all-start.2
  175.5 38.3 %all-to-all-start = ((bf16[512,8,128]{2,0,1:T(8,128)(2,1)}), bf16[512,8,128]{2,0,1:T(8,128)(2,1)}, u32[]{:S(2)}, u32[]{:S(2)}) async-start(bf16[512,8,128]{2,0,1:T(8,128)(2,1)} %fusion.92), calls=%async_computation | async-start | bytes 2097152 | tf_op jit(solution)/shard_map/all_to_all | solution.py:114
  179.7 132.9 %all-gather.16.cloned.1.call-start = ((), (), s32[]{:S(2)}) async-start(), calls=%async_computation.18 | async-start | bytes 4456448 | tf_op jit(solution)/shard_map/all_gather | solution.py:95
  180.3 245.5 %all-reduce.18.cloned.1.call-start = ((), (), s32[]{:S(2)}) async-start(), calls=%async_computation.19 | async-start | bytes 8388608 | tf_op jit(solution)/shard_map/psum | solution.py:157
  319.6 208.8 %all-gather.18.cloned.1.call-start = ((), (), s32[]{:S(2)}) async-start(), calls=%async_computation.20 | async-start | bytes 13369344 | tf_op jit(solution)/shard_map/all_gather | solution.py:160
  320.2 309.2 %all-gather.20.cloned.1.call-start = ((), (), s32[]{:S(2)}) async-start(), calls=%async_computation.21 | async-start | bytes 13369344 | tf_op jit(solution)/shard_map/all_gather | solution.py:161
  320.9 409.5 %all-gather.22.cloned.1.call-start = ((), (), s32[]{:S(2)}) async-start(), calls=%async_computation.22 | async-start | bytes 13369344 | tf_op jit(solution)/shard_map/all_gather | solution.py:162
  321.7 556.9 %all-reduce.22.cloned.1.call-start = ((), (), s32[]{:S(2)}) async-start(), calls=%async_computation.24 | async-start | bytes 8388608 | tf_op jit(solution)/shard_map/psum | solution.py:180
  431.0 97.4 %copy-start.22 = (bf16[512,2048]{1,0:T(8,128)(2,1)}, bf16[512,2048]{1,0:T(8,128)(2,1)S(1)}, u32[]{:S(2)}) copy-start(bf16[512,2048]{1,0:T(8,128)(2,1)S(1)} %multiply_convert_fusion.3) | copy-start | bytes 6291460
  539.7 190.8 %copy-start.20 = (bf16[512,2048]{1,0:T(8,128)(2,1)S(1)}, bf16[512,2048]{1,0:T(8,128)(2,1)}, u32[]{:S(2)}) copy-start(bf16[512,2048]{1,0:T(8,128)(2,1)} %param.21) | copy-start | bytes 6291460
  772.2 172.1 %all-reduce.20.cloned.1.call-start = ((), (), s32[]{:S(2)}) async-start(), calls=%async_computation.23 | async-start | bytes 4194304 | tf_op jit(solution)/shard_map/psum | solution.py:173
  953.9 30.6 %all-to-all-start.4 = ((bf16[512,8,128]{2,0,1:T(8,128)(2,1)}), bf16[512,8,128]{2,0,1:T(8,128)(2,1)S(1)}, u32[]{:S(2)}, u32[]{:S(2)}) async-start(bf16[512,8,128]{2,0,1:T(8,128)(2,1)} %bitcast.303), calls=%async_computation.4 | async-start | bytes 2097152 | tf_op jit(solution)/shard_map/all_to_all | solution.py:190
  1106.9 17.5 all-to-all-start.6
  1124.3 18.4 all-to-all-start.7
  1142.8 29.6 %all-to-all-start.5 = ((bf16[2048,2,128]{2,1,0:T(2,128)(2,1)}), bf16[2048,2,128]{2,1,0:T(2,128)(2,1)}, u32[]{:S(2)}, u32[]{:S(2)}) async-start(bf16[2048,2,128]{2,1,0:T(2,128)(2,1)} %copy.191), calls=%async_computation.5 | async-start | bytes 2097152 | tf_op jit(solution)/shard_map/all_to_all | solution.py:223
  1147.1 147.9 %all-reduce.24.cloned.1.call-start = ((), (), s32[]{:S(2)}) async-start(), calls=%async_computation.25 | async-start | bytes 8388608 | tf_op jit(solution)/shard_map/psum | solution.py:239
  1188.8 353.7 %reduce-scatter.20.cloned.1.call-start = ((), (), s32[]{:S(2)}) async-start(), calls=%async_computation.32 | async-start | bytes 26738688 | tf_op jit(solution)/shard_map/reduce_scatter | solution.py:266
  1204.6 414.2 %reduce-scatter.10.cloned.1.call-start = ((), (), s32[]{:S(2)}) async-start(), calls=%async_computation.27 | async-start | bytes 4456448 | tf_op jit(solution)/shard_map/reduce_scatter | solution.py:250
  1209.8 485.2 %reduce-scatter.12.cloned.1.call-start = ((), (), s32[]{:S(2)}) async-start(), calls=%async_computation.28 | async-start | bytes 4456448 | tf_op jit(solution)/shard_map/reduce_scatter | solution.py:253
  1213.3 588.7 %reduce-scatter.14.cloned.1.call-start = ((), (), s32[]{:S(2)}) async-start(), calls=%async_computation.29 | async-start | bytes 8912896 | tf_op jit(solution)/shard_map/reduce_scatter | solution.py:256
  1222.5 687.1 %reduce-scatter.8.cloned.1.call-start = ((), (), s32[]{:S(2)}) async-start(), calls=%async_computation.26 | async-start | bytes 8912896 | tf_op jit(solution)/shard_map/reduce_scatter | solution.py:247
  1229.6 927.8 %reduce-scatter.16.cloned.1.call-start = ((), (), s32[]{:S(2)}) async-start(), calls=%async_computation.30 | async-start | bytes 26738688 | tf_op jit(solution)/shard_map/reduce_scatter | solution.py:260
  1244.0 1160.6 %reduce-scatter.18.cloned.1.call-start = ((), (), s32[]{:S(2)}) async-start(), calls=%async_computation.31 | async-start | bytes 26738688 | tf_op jit(solution)/shard_map/reduce_scatter | solution.py:263
  1258.3 110.4 %copy-start.43 = (f32[512]{0:T(512)S(1)}, f32[512]{0:T(512)}, u32[]{:S(2)}) copy-start(f32[512]{0:T(512)} %copy-done.42) | copy-start | bytes 6148
  (51 other events, 483.9 us)
Sparse Core Ops, SparseCore 0:
  10.2 44.3 all-gather.11
  56.8 41.7 all-gather.13
  100.9 48.0 all-gather.9
  182.5 57.7 all-gather.15
  319.7 106.0 all-reduce.17
  427.9 100.4 all-gather.17
  530.7 98.6 all-gather.19
  631.7 98.6 all-gather.21
  772.3 106.1 all-reduce.21
  881.3 62.9 all-reduce.19
  1188.9 106.0 all-reduce.23
  1298.9 243.5 reduce-scatter.19
  1546.9 71.8 reduce-scatter.9
  1623.1 71.7 reduce-scatter.11
  1699.4 102.5 reduce-scatter.13
  1806.5 103.0 reduce-scatter.7
  1914.1 243.1 reduce-scatter.15
  2161.9 242.6 reduce-scatter.17
where the time goes:
time: 2420 us; the launch traced here: 2410 us
  waiting for transfers between devices  1730 us (71%)
  matrix products  275 us (11%)
  blocking collectives  189 us (8%)
  other arithmetic  103 us (4%)
  local copies, waits for them, and re-layouts  55.2 us (2%)
  starting transfers between devices  30.1 us (1%)
    reduce_scatter x1, waiting for transfers between devices, body(): lax.psum_scatter(contract_first(normed_two, d_gate), ('fsdp', 'ctx'), sca...  248 us
    reduce_scatter x1, waiting for transfers between devices, body(): lax.psum_scatter(contract_first(normed_two, d_up), ('fsdp', 'ctx'), scatt...  247 us
    reduce_scatter x1, waiting for transfers between devices, body(): lax.psum_scatter(contract_first(cotangent, hidden), ('fsdp', 'ctx'), scat...  168 us
    reduce_scatter x1, waiting for transfers between devices, body(): lax.psum_scatter(contract_first(normed_bf, dq_flat), ('fsdp', 'ctx'), sca...  108 us
    reduce_scatter x1, waiting for transfers between devices, body(): lax.psum_scatter(contract_first(d_branch, o_tok), ('fsdp', 'ctx'), scatte...  107 us
    all_gather x1, waiting for transfers between devices, body(): lax.all_gather(w_gate, ('fsdp', 'ctx'), axis=0, tiled=True)  97.4 us
    psum x1, waiting for transfers between devices, body(): lax.psum(contract_last(d_gate, wg_full) + contract_last(d_up, wu_full), '...  94.6 us
    unnamed x2, blocking collectives  92.6 us
  transfers between devices with their start and end apart: 25, of which 22 were waited for; matrix products, arithmetic and copies ran while one was open for 10% of the time, Pallas kernels for 0%

commit v1 on v0

v1 whole, which is shorter than its diff:
```python
import functools

import jax
import jax.numpy as jnp
from jax import lax
from jax.experimental import pallas as pl
from jax.experimental.pallas import tpu as pltpu
from jax.experimental.layout import Layout, with_layout_constraint
from jax.sharding import PartitionSpec as P


HEAD_SIZE = 128


EPS = 1e-06
THETA = 1000000.0
MASK_FILL = -1e30
BOTH = ("fsdp", "ctx")
SIDE = 128
TAIL = 16
PIECE = 256
ROW_MAJOR = Layout(major_to_minor=(0, 1))


def rms_scale(features, gain_vec):
    inverse = lax.rsqrt(jnp.mean(features * features, axis=-1, keepdims=True) + EPS)
    return features * inverse * gain_vec


def rotate(features, cosine, sine):
    half_width = features.shape[-1] // 2
    turned = jnp.concatenate([-features[..., half_width:], features[..., :half_width]], axis=-1)
    return features * cosine + turned * sine


def rope_tables(positions, width):
    half_width = width // 2
    frequency = THETA ** (-(jnp.arange(half_width, dtype=jnp.float32) * 2.0 / width))
    angles = positions[:, None] * frequency[None, :]
    angles = jnp.concatenate([angles, angles], axis=-1)
    return (jnp.cos(angles)[:, None, :], jnp.sin(angles)[:, None, :])


def contract_last(left_side, right_side):
    return lax.dot_general(
        left_side, right_side, (((1,), (1,)), ((), ())), preferred_element_type=jnp.float32
    )


def contract_first(left_side, right_side):
    return lax.dot_general(
        left_side, right_side, (((0,), (0,)), ((), ())), preferred_element_type=jnp.float32
    )


def pair_sum(part, after=None):
    mine = part.astype(jnp.bfloat16)
    count = lax.axis_size("tp")
    total = mine.astype(jnp.float32)
    for step in range(1, count):
        ring = [(i, (i + step) % count) for i in range(count)]
        other = lax.ppermute(mine, "tp", ring)
        if after is not None:
            other, _ = lax.optimization_barrier((other, after))
        total = total + other.astype(jnp.float32)
    return total


def ring_order():
    outer, inner = lax.axis_size("fsdp"), lax.axis_size("ctx")
    cores = 2 if outer % 2 == 0 else 1
    lines = outer // cores
    chips = [(line, 0) for line in range(lines)]
    for turn, line in enumerate(reversed(range(lines))):
        across = range(1, inner) if turn % 2 == 0 else range(inner - 1, 0, -1)
        chips += [(line, place) for place in across]
    return [(line * cores + core) * inner + place for line, place in chips for core in range(cores)]


def take_blocks(features, order):
    size = features.shape[1] // len(order)
    return jnp.concatenate([features[:, i * size : (i + 1) * size] for i in order], axis=1)


def scatter_sum(part):
    return lax.psum_scatter(
        part, BOTH, scatter_dimension=0, tiled=True, axis_index_groups=[ring_order()]
    )


def gather_rows(shard):
    return lax.all_gather(shard, BOTH, axis=0, tiled=True, axis_index_groups=[ring_order()])


def swap_ctx(planes):
    return lax.all_to_all(planes, "ctx", split_axis=0, concat_axis=0, tiled=True)


def rope_kernel(q_heads, kv_heads, raw, cosine, sine, q_gain, k_gain, planes):
    count = planes.shape[0]
    for plane in range(count):
        sources = [plane * q_heads + h for h in range(q_heads)]
        sources += [count * q_heads + plane * kv_heads + h for h in range(kv_heads)]
        for i, source in enumerate(sources):
            gain = q_gain if i < q_heads else k_gain
            rows = raw[:, source * HEAD_SIZE : (source + 1) * HEAD_SIZE]
            scaled = rms_scale(rows, gain[...])
            turned = pltpu.roll(scaled, HEAD_SIZE // 2, 1)
            result = scaled * cosine[...] + turned * sine[...]
            planes[plane, :, i * HEAD_SIZE : (i + 1) * HEAD_SIZE] = result.astype(jnp.bfloat16)
        first = (count * (q_heads + kv_heads) + plane * kv_heads) * HEAD_SIZE
        wide = kv_heads * HEAD_SIZE
        values = raw[:, first : first + wide].astype(jnp.bfloat16)
        planes[plane, :, len(sources) * HEAD_SIZE :] = values


def to_heads(flat):
    count = lax.axis_size("ctx")
    return join_planes(flat.reshape(flat.shape[0], count, -1).transpose(1, 0, 2))


def join_planes(planes):
    moved = swap_ctx(planes)
    return moved.reshape(-1, moved.shape[2])


def to_tokens(joined, widths):
    count = lax.axis_size("ctx")
    moved = swap_ctx(joined.reshape(count, -1, joined.shape[1]))
    ends = [sum(widths[: i + 1]) for i in range(len(widths))]
    return [
        moved[:, :, end - wide : end].transpose(1, 0, 2).reshape(moved.shape[1], -1)
        for end, wide in zip(ends, widths)
    ]


def block_mask(low, start_col, start_row, piece_col, piece_row):
    rows = pl.ds(low, PIECE)
    own_start = start_col[rows, :]
    same = own_start == start_row[:, :low] if low else None
    left = lax.broadcasted_iota(jnp.int32, (PIECE, PIECE), 0)
    right = lax.broadcasted_iota(jnp.int32, (PIECE, PIECE), 1)
    own_piece = piece_col[rows, :]
    near = (right <= left) | ((own_piece == piece_row[:, low : low + PIECE]) & (own_piece > 0))
    near = near & ((own_start == start_row[:, low : low + PIECE]) | (left == right))
    return near if same is None else jnp.concatenate([same, near], axis=1)


def head_cols(ref, rows, heads):
    return jnp.concatenate(
        [ref[rows, h * HEAD_SIZE : (h + 1) * HEAD_SIZE] for h in heads], axis=0
    )


def masked_scores(q_rows, k_rows, mask, group):
    scores = contract_last(q_rows, k_rows) * HEAD_SIZE ** (-0.5)
    return jnp.where(jnp.concatenate([mask] * group, axis=0), scores, MASK_FILL)


def forward_kernel(q_heads, kv_heads, qkv, start_col, start_row, piece_col, piece_row, out, lse):
    group = q_heads // kv_heads
    for low in range(0, qkv.shape[0], PIECE):
        rows, high = pl.ds(low, PIECE), low + PIECE
        mask = block_mask(low, start_col, start_row, piece_col, piece_row)
        for c in range(kv_heads):
            heads = range(c * group, (c + 1) * group)
            k_rows = head_cols(qkv, pl.ds(0, high), [q_heads + c])
            v_rows = head_cols(qkv, pl.ds(0, high), [q_heads + kv_heads + c])
            scores = masked_scores(head_cols(qkv, rows, heads), k_rows, mask, group)
            row_max = jnp.max(scores, axis=-1, keepdims=True)
            expo = jnp.exp(scores - row_max)
            total = jnp.sum(expo, axis=-1, keepdims=True)
            probs = (expo * (1.0 / total)).astype(jnp.bfloat16)
            result = jnp.dot(probs, v_rows, preferred_element_type=jnp.float32)
            log_total = row_max + jnp.log(total)
            for i, h in enumerate(heads):
                part = slice(i * PIECE, (i + 1) * PIECE)
                out[rows, h * HEAD_SIZE : (h + 1) * HEAD_SIZE] = result[part].astype(jnp.bfloat16)
                lse[rows, h : h + 1] = log_total[part]


def backward_kernel(
    q_heads, kv_heads, qkv, d_out, lse, start_col, start_row, piece_col, piece_row, grads, k_sum, v_sum
):
    group = q_heads // kv_heads
    scale = HEAD_SIZE ** (-0.5)
    k_sum[...] = jnp.zeros_like(k_sum)
    v_sum[...] = jnp.zeros_like(v_sum)
    for low in range(0, qkv.shape[0], PIECE):
        rows, high = pl.ds(low, PIECE), low + PIECE
        mask = block_mask(low, start_col, start_row, piece_col, piece_row)
        for c in range(kv_heads):
            heads = range(c * group, (c + 1) * group)
            keys = pl.ds(0, high)
            k_rows = head_cols(qkv, keys, [q_heads + c])
            v_rows = head_cols(qkv, keys, [q_heads + kv_heads + c])
            q_rows = head_cols(qkv, rows, heads)
            d_rows = head_cols(d_out, rows, heads)
            totals = jnp.concatenate([lse[rows, h : h + 1] for h in heads], axis=0)
            probs = jnp.exp(masked_scores(q_rows, k_rows, mask, group) - totals)
            d_probs = contract_last(d_rows, v_rows)
            delta = jnp.sum(probs * d_probs, axis=-1, keepdims=True)
            d_scores = (probs * (d_probs - delta)).astype(jnp.bfloat16)
            d_query = jnp.dot(d_scores, k_rows, preferred_element_type=jnp.float32) * scale
            for i, h in enumerate(heads):
                part = d_query[i * PIECE : (i + 1) * PIECE]
                grads[rows, h * HEAD_SIZE : (h + 1) * HEAD_SIZE] = part.astype(jnp.bfloat16)
            cols = slice(c * HEAD_SIZE, (c + 1) * HEAD_SIZE)
            k_sum[keys, cols] += contract_first(d_scores, q_rows)
            v_sum[keys, cols] += contract_first(probs.astype(jnp.bfloat16), d_rows)
    middle = (q_heads + kv_heads) * HEAD_SIZE
    grads[:, q_heads * HEAD_SIZE : middle] = (k_sum[...] * scale).astype(jnp.bfloat16)
    grads[:, middle:] = v_sum[...].astype(jnp.bfloat16)


def attention_call(kernel, results, scratch, work, args):
    rows, heads = args[0].shape[0], work
    pairs = rows * (rows + PIECE) // 2 * heads
    return pl.pallas_call(
        kernel,
        out_shape=results,
        in_specs=[pl.BlockSpec(memory_space=pltpu.VMEM)] * len(args),
        out_specs=[pl.BlockSpec(memory_space=pltpu.VMEM)] * len(results),
        scratch_shapes=scratch,
        cost_estimate=pl.CostEstimate(
            flops=pairs * HEAD_SIZE * 16,
            transcendentals=pairs,
            bytes_accessed=sum(a.size * a.dtype.itemsize for a in args),
        ),
        compiler_params=pltpu.CompilerParams(vmem_limit_bytes=56 * 1024 * 1024),
    )(*args)


def body(
    tokens,
    cotangent,
    sequence_begin,
    piece,
    padding_length,
    attn_gain,
    q_gain,
    k_gain,
    w_query,
    key_weight,
    value_weight,
    w_out,
    mlp_gain,
    w_gate,
    w_up,
    w_down,
):
    f32 = jnp.float32
    bf16 = jnp.bfloat16
    tok_rows = tokens.shape[0]
    group_rows = sequence_begin.shape[0]
    offset = lax.axis_index("ctx") * tok_rows
    local_index = offset + jnp.arange(tok_rows, dtype=jnp.int32)
    my_start = lax.dynamic_slice_in_dim(sequence_begin, offset, tok_rows)
    cosine, sine = rope_tables((local_index - my_start).astype(f32), HEAD_SIZE)
    key_index = jnp.arange(group_rows, dtype=jnp.int32)
    key_live = key_index < group_rows - padding_length[0]

    def head_prep(raw_heads, gain_vec):
        return rotate(rms_scale(raw_heads, gain_vec), cosine, sine)

    order = ring_order()
    back = [order.index(i) for i in range(len(order))]
    place = (jnp.array(order)[:, None] == jnp.arange(len(order))[None, :]).astype(f32)
    tokens = take_blocks(tokens, order)
    cotangent = take_blocks(cotangent, order)
    width = tokens.shape[1]
    tp_cols = w_query.shape[1]
    kv_cols = key_weight.shape[1]
    qkv_cols = tp_cols + 2 * kv_cols
    rows = attn_gain.shape[0]
    ff_cols = w_gate.shape[1]
    small = q_gain.shape[0]
    side_index = lax.broadcasted_iota(jnp.int32, (rows, SIDE), 1)
    side = jnp.zeros((rows, SIDE), bf16)
    short = ((0, rows - small),)
    gains = (attn_gain, mlp_gain, jnp.pad(q_gain, short), jnp.pad(k_gain, short))
    for i, gain in enumerate(gains):
        side = jnp.where(side_index == i, gain[:, None], side)
    shards = width // rows
    w_qkv = jnp.concatenate([w_query, key_weight, value_weight, side], axis=1)
    qkv_full = gather_rows(w_qkv)
    wo_full = gather_rows(w_out)
    gu_full = gather_rows(jnp.concatenate([w_gate, w_up], axis=1))
    wd_full = gather_rows(w_down)
    side_full = qkv_full[:, qkv_cols:]
    g_attn, g_mlp = side_full[:, 0], side_full[:, 1]
    head_side = side_full.reshape(shards, rows, SIDE)[:, :small, 2:4]
    head_side = jnp.sum(place[:, :, None, None] * head_side[:, None].astype(f32), axis=0)
    g_query = head_side[..., 0].reshape(-1)
    g_key = head_side[..., 1].reshape(-1)
    attn_gain_f = g_attn.astype(f32)
    qgain_f = g_query.astype(f32)
    kgain_f = g_key.astype(f32)
    x_rows = tokens.astype(f32)
    normed_bf = rms_scale(x_rows, attn_gain_f).astype(bf16)
    qkv_raw = jnp.dot(normed_bf, qkv_full, preferred_element_type=f32)
    q_raw = qkv_raw[:, :tp_cols].reshape(tok_rows, -1, HEAD_SIZE)
    key_unrotated = qkv_raw[:, tp_cols : tp_cols + kv_cols].reshape(tok_rows, -1, HEAD_SIZE)
    ctx_count = lax.axis_size("ctx")
    q_wide, kv_wide = tp_cols // ctx_count, kv_cols // ctx_count
    q_heads, kv_heads = q_wide // HEAD_SIZE, kv_wide // HEAD_SIZE
    lower = jnp.arange(HEAD_SIZE) < HEAD_SIZE // 2
    planes = pl.pallas_call(
        functools.partial(rope_kernel, q_heads, kv_heads),
        name="rope",
        out_shape=jax.ShapeDtypeStruct((ctx_count, tok_rows, q_wide + 2 * kv_wide), bf16),
        in_specs=[pl.BlockSpec(memory_space=pltpu.VMEM)] * 5,
        out_specs=pl.BlockSpec(memory_space=pltpu.VMEM),
        cost_estimate=pl.CostEstimate(
            flops=16 * qkv_raw.size, transcendentals=0, bytes_accessed=6 * qkv_raw.size
        ),
    )(
        qkv_raw,
        cosine[:, 0],
        jnp.where(lower, -sine[:, 0], sine[:, 0]),
        qgain_f[None],
        kgain_f[None],
    )
    joined = join_planes(planes)
    masks = (
        sequence_begin[:, None],
        jnp.where(key_live, sequence_begin, -1)[None, :],
        piece[:, None],
        piece[None, :],
    )
    o_head, log_totals = attention_call(
        functools.partial(forward_kernel, q_heads, kv_heads),
        [
            jax.ShapeDtypeStruct((group_rows, q_wide), bf16),
            jax.ShapeDtypeStruct((group_rows, q_heads), f32),
        ],
        [],
        q_heads,
        (joined, *masks),
    )
    (o_tok,) = to_tokens(o_head, [q_wide])
    residual = x_rows + pair_sum(contract_last(o_tok, wo_full))
    mlp_gain_f = g_mlp.astype(f32)
    normed_two = rms_scale(residual, mlp_gain_f).astype(bf16)
    gate_up = jnp.dot(normed_two, gu_full, preferred_element_type=f32)
    gate_value = gate_up[:, :ff_cols]
    up_value = gate_up[:, ff_cols:]
    gate_sigmoid = jax.nn.sigmoid(gate_value)
    gate_silu = gate_value * gate_sigmoid
    hidden = (gate_silu * up_value).astype(bf16)
    down_part = contract_last(hidden, wd_full).astype(bf16)
    grad_down_part = with_layout_constraint(
        contract_first(cotangent, hidden).astype(bf16), ROW_MAJOR
    )
    grad_down_part, cotangent = lax.optimization_barrier((grad_down_part, cotangent))
    grad_down = scatter_sum(grad_down_part)
    d_hidden = jnp.dot(cotangent, wd_full, preferred_element_type=f32)
    d_gate = (
        d_hidden * up_value * gate_sigmoid * (1.0 + gate_value * (1.0 - gate_sigmoid))
    ).astype(bf16)
    d_up = (d_hidden * gate_silu).astype(bf16)
    d_gate_up = jnp.concatenate([d_gate, d_up], axis=1)
    grad_gate_up_part = contract_first(normed_two, d_gate_up).astype(bf16)
    d_norm_two = pair_sum(contract_last(d_gate_up, gu_full))
    grad_gate_up_part, down_part, d_norm_two = lax.optimization_barrier(
        (grad_gate_up_part, down_part, d_norm_two)
    )
    grad_gate_up = scatter_sum(grad_gate_up_part)
    layer_out = residual + pair_sum(down_part)
    layer_out = take_blocks(layer_out.astype(bf16), back)
    _, pull_two = jax.vjp(rms_scale, residual, mlp_gain_f)
    d_residual, d_mlp_gain = pull_two(d_norm_two)
    d_residual = d_residual + cotangent.astype(f32)
    d_branch = d_residual.astype(bf16)
    grad_out_part = contract_first(d_branch, o_tok).astype(bf16)
    grad_out_part, d_branch = lax.optimization_barrier((grad_out_part, d_branch))
    grad_out = scatter_sum(grad_out_part)
    d_out = (
        jnp.dot(d_branch, wo_full, preferred_element_type=f32)
        .astype(bf16)
    )
    d_head = to_heads(d_out)

    (d_joined,) = attention_call(
        functools.partial(backward_kernel, q_heads, kv_heads),
        [jax.ShapeDtypeStruct(joined.shape, bf16)],
        [pltpu.VMEM((group_rows, kv_wide), f32)] * 2,
        q_heads,
        (joined, d_head, log_totals, *masks),
    )
    dq_tok, dk_tok, dv_flat = to_tokens(d_joined, [q_wide, kv_wide, kv_wide])
    dq_tok = dq_tok.reshape(tok_rows, -1, HEAD_SIZE)
    dk_tok = dk_tok.reshape(tok_rows, -1, HEAD_SIZE)
    _, pull_query = jax.vjp(head_prep, q_raw, qgain_f)
    dq_raw, d_qgain = pull_query(dq_tok.astype(f32))
    _, pull_key = jax.vjp(head_prep, key_unrotated, kgain_f)
    dk_raw, d_kgain = pull_key(dk_tok.astype(f32))
    dq_flat = dq_raw.astype(bf16).reshape(tok_rows, -1)
    dk_flat = dk_raw.astype(bf16).reshape(tok_rows, -1)
    picks = (jnp.arange(TAIL)[:, None] == jnp.arange(SIDE)[None, :]).astype(bf16)
    d_qkv = jnp.concatenate(
        [
            jnp.concatenate([part, jnp.zeros((TAIL, part.shape[1]), bf16)], axis=0)
            for part in (dq_flat, dk_flat, dv_flat)
        ]
        + [jnp.concatenate([jnp.zeros((tok_rows, SIDE), bf16), picks], axis=0)],
        axis=1,
    )
    d_norm_part = contract_last(d_qkv, qkv_full)[:tok_rows].astype(bf16)
    _, pull_one = jax.vjp(rms_scale, x_rows, attn_gain_f)
    _, d_attn_gain = pull_one(d_norm_part.astype(f32))
    d_norm = pair_sum(d_norm_part, d_attn_gain)
    d_tokens, _ = pull_one(d_norm)
    grad_tokens = take_blocks((d_residual + d_tokens).astype(bf16), back)
    head_grads = jnp.stack([d_qgain, d_kgain]).reshape(2, 1, shards, small)
    head_grads = jnp.sum(place[None, :, :, None] * head_grads, axis=2)
    head_grads = jnp.pad(head_grads, ((0, 0), (0, 0), (0, rows - small)))
    gain_rows = jnp.concatenate(
        [d_attn_gain[None], d_mlp_gain[None] / lax.axis_size("tp"), head_grads.reshape(2, width)]
    )
    gain_rows = jnp.pad(gain_rows, ((0, TAIL - 4), (0, 0)))
    gain_rows = pair_sum(gain_rows)
    normed_tail = jnp.concatenate([normed_bf, gain_rows.astype(bf16)], axis=0)
    grad_qkv_part = contract_first(normed_tail, d_qkv).astype(bf16)
    grad_qkv_part = with_layout_constraint(grad_qkv_part, ROW_MAJOR)
    grad_qkv = scatter_sum(grad_qkv_part)
    grad_side = grad_qkv[:, qkv_cols:]
    side_sums = grad_side[:, :4].astype(f32)
    return (
        layer_out,
        grad_tokens,
        side_sums[:, 0],
        side_sums[:small, 2],
        side_sums[:small, 3],
        grad_qkv[:, :tp_cols].astype(f32),
        grad_qkv[:, tp_cols : tp_cols + kv_cols].astype(f32),
        grad_qkv[:, tp_cols + kv_cols : qkv_cols].astype(f32),
        grad_out.astype(f32),
        grad_side[:, 1].astype(f32),
        grad_gate_up[:, :ff_cols].astype(f32),
        grad_gate_up[:, ff_cols:].astype(f32),
        grad_down.astype(f32),
    )


def solution(mesh):
    in_specs = (
        P(("fsdp", "ctx"), None),
        P(("fsdp", "ctx"), None),
        P("fsdp"),
        P("fsdp"),
        P("fsdp"),
        P(("fsdp", "ctx")),
        P(("fsdp", "ctx")),
        P(("fsdp", "ctx")),
        P(("fsdp", "ctx"), "tp"),
        P(("fsdp", "ctx"), "tp"),
        P(("fsdp", "ctx"), "tp"),
        P(("fsdp", "ctx"), "tp"),
        P(("fsdp", "ctx")),
        P(("fsdp", "ctx"), "tp"),
        P(("fsdp", "ctx"), "tp"),
        P(("fsdp", "ctx"), "tp"),
    )
    out_specs = (
        P(("fsdp", "ctx"), None),
        P(("fsdp", "ctx"), None),
        P(("fsdp", "ctx")),
        P(("fsdp", "ctx")),
        P(("fsdp", "ctx")),
        P(("fsdp", "ctx"), "tp"),
        P(("fsdp", "ctx"), "tp"),
        P(("fsdp", "ctx"), "tp"),
        P(("fsdp", "ctx"), "tp"),
        P(("fsdp", "ctx")),
        P(("fsdp", "ctx"), "tp"),
        P(("fsdp", "ctx"), "tp"),
        P(("fsdp", "ctx"), "tp"),
    )

    return jax.shard_map(body, mesh=mesh, in_specs=in_specs, out_specs=out_specs, check_vma=False)
```

time: 2420 us -> 898 us (0.37)
  waiting for transfers between devices: 1730 us -> 499 us
  blocking collectives: 189 us -> 29.8 us
  matrix products: 275 us -> 146 us
  Pallas kernels: 0 us -> 41.9 us
  other arithmetic: 103 us -> 62.7 us
    reduce_scatter x7 -> x4, waiting for transfers between devices: 1030 us -> 148 us  [scatter_sum(): lax.psum_scatter(part, BOTH, scatter_dimension=0, tiled=True, axis_index_...]
    psum x4 -> x0, waiting for transfers between devices: 266 us -> none  [the longest x1 94.6 us: body(): lax.psum(contract_last(d_gate, wg_full) + contract_last(d_up, wu_full), '...]
    all_gather x7 -> x4, waiting for transfers between devices: 330 us -> 82.7 us  [gather_rows(): lax.all_gather(shard, BOTH, axis=0, tiled=True, axis_index_groups=[ring_o...]
    ppermute x0 -> x5, waiting for transfers between devices: none -> 139 us  [pair_sum(): other = lax.ppermute(mine, 'tp', ring)]
    dot_general x34 -> x3, matrix products: 140 us -> 37.5 us  [the longest x1 21.9 us: body(): gate_up = jnp.dot(normed_two, gu_full, preferred_element_type=f32)]
    unnamed x2 -> x0, blocking collectives: 92.6 us -> none
    all_gather x2 -> x0, blocking collectives: 63 us -> none  [the longest x1 34.1 us: body(): lax.all_gather(attn_gain, ('fsdp', 'ctx'), axis=0, tiled=True)]
    pallas_call x0 -> x3, Pallas kernels: none -> 41.9 us  [the longest x2 36 us: attention_call(): pl.pallas_call(kernel, out_shape=results, in_specs=[pl.BlockSpec(memory_s...]
  transfers between devices with their start and end apart: 25 -> 16, of which waited for: 22 -> 13; matrix products, arithmetic and copies ran while one was open for 10% -> 24% of each run, Pallas kernels for 0% -> 2%
where the time goes in v1:
time: 898 us; the launch traced here: 890 us
  waiting for transfers between devices  499 us (56%)
  matrix products  146 us (16%)
  local copies, waits for them, and re-layouts  74 us (8%)
  other arithmetic  62.7 us (7%)
  Pallas kernels  41.9 us (5%)
  blocking collectives  29.8 us (3%)
  starting transfers between devices  20.9 us (2%)
  between operations  16.3 us (2%)
    reduce_scatter x4, waiting for transfers between devices, scatter_sum(): lax.psum_scatter(part, BOTH, scatter_dimension=0, tiled=True, axis_index_...  148 us
    ppermute x5, waiting for transfers between devices, pair_sum(): other = lax.ppermute(mine, 'tp', ring)  139 us
    all_to_all x3, waiting for transfers between devices, swap_ctx(): lax.all_to_all(planes, 'ctx', split_axis=0, concat_axis=0, tiled=True)  126 us
    all_gather x4, waiting for transfers between devices, gather_rows(): lax.all_gather(shard, BOTH, axis=0, tiled=True, axis_index_groups=[ring_o...  82.7 us
    unnamed x149, local copies, waits for them, and re-layouts  49.4 us
    dot_general x4, matrix products, contract_first(): lax.dot_general(left_side, right_side, (((0,), (0,)), ((), ())), preferre...  49 us
    dot_general x4, matrix products, contract_last(): lax.dot_general(left_side, right_side, (((1,), (1,)), ((), ())), preferre...  44.9 us
    pallas_call x2, Pallas kernels, attention_call(): pl.pallas_call(kernel, out_shape=results, in_specs=[pl.BlockSpec(memory_s...  36 us
  transfers between devices with their start and end apart: 16, of which 13 were waited for; matrix products, arithmetic and copies ran while one was open for 24% of the time, Pallas kernels for 2%

profile of v1, /device:TPU:0, one launch (start us, length us, event | category | flops | bytes accessed | tf_op | source)
XLA Modules:
  0.0 890.1 jit_solution(2964629103545193167)
XLA Ops:
  32.2 34.1 %all-gather.5.cloned.1.call-done = bf16[2048,2176]{1,0:T(8,128)(2,1)} async-done(((bf16[128,2176]{1,0:T(8,128)(2,1)}), bf16[2048,2176]{1,0:T(8,128)(2,1)}) %all-gather.5.cloned.1.call-update) | async-done | bytes 8912912 | tf_op jit(solution)/shard_map/all_gather | solution.py:92
  72.2 11.1 %fusion.53.raw = f32[512,2176]{1,0:T(8,128)} fusion(bf16[512,2048]{1,0:T(8,128)(2,1)S(1)} %fusion.7, bf16[2048,2176]{1,0:T(8,128)(2,1)} %all-gather.5.cloned.1.call-done), kind=kOutput, calls=%fused_computation.210 | convolution fusion | flops 4563402752 | bytes 15466496 | tf_op jit(solution)/shard_map/dot_general | solution.py:301
  83.3 5.9 rope.1
  89.2 4.9 all-to-all-start
  98.0 57.1 %all-to-all-done = bf16[4,512,512]{2,1,0:T(8,128)(2,1)} async-done(((bf16[4,512,512]{2,1,0:T(8,128)(2,1)}), bf16[4,512,512]{2,1,0:T(8,128)(2,1)}, u32[]{:S(2)}, u32[]{:S(2)}) %all-to-all-start) | async-done | bytes 2097184 | tf_op jit(solution)/shard_map/all_to_all | solution.py:96
  155.1 14.6 %shard_map.264 = (bf16[2048,256]{1,0:T(8,128)(2,1)}, f32[2048,2]{1,0:T(8,128)}) custom-call(bf16[2048,512]{1,0:T(8,128)(2,1)} %bitcast.1.qkv, s32[2048,1]{1,0:T(8,128)} %copy.157.start_col, s32[1,2048]{1,0:T(1,128)} %bitcast.101, s32[2048,1]{1,0:T(8,128)} %copy.158.piece_col, s32[1,2048]{1,0:T(1,128)} %bitcast.98), custom_call_target="tpu_custom_call" | custom-call | flops 9663676416 | bytes 2129920 | tf_op jit(solution)/shard_map/pallas_call | solution.py:219
  185.8 27.6 %all-to-all-done.1 = bf16[4,512,256]{1,2,0:T(8,128)(2,1)S(1)} async-done(((bf16[4,512,256]{1,2,0:T(8,128)(2,1)}), bf16[4,512,256]{1,2,0:T(8,128)(2,1)S(1)}, u32[]{:S(2)}, u32[]{:S(2)}) %all-to-all-start.1) | async-done | bytes 1048608 | tf_op jit(solution)/shard_map/all_to_all | solution.py:96
  213.4 5.0 convolution_convert_fusion.5
  226.9 36.3 %collective-permute-done = bf16[512,2048]{1,0:T(8,128)(2,1)S(1)} collective-permute-done((bf16[512,2048]{1,0:T(8,128)(2,1)S(1)}, bf16[512,2048]{1,0:T(8,128)(2,1)S(1)}, u32[]{:S(2)}, u32[]{:S(2)}) %collective-permute-start) | collective-permute-done | bytes 2097184 | tf_op jit(solution)/shard_map/ppermute | solution.py:62
  266.3 9.6 %all-gather.9.cloned.1.call-done = bf16[2048,6144]{1,0:T(8,128)(2,1)} async-done(((bf16[128,6144]{1,0:T(8,128)(2,1)}), bf16[2048,6144]{1,0:T(8,128)(2,1)}) %all-gather.9.cloned.1.call-update) | async-done | bytes 25165840 | tf_op jit(solution)/shard_map/all_gather | solution.py:92
  275.9 21.9 %fusion.45 = f32[512,6144]{1,0:T(8,128)} fusion(bf16[2048,6144]{1,0:T(8,128)(2,1)} %all-gather.9.cloned.1.call-done, f32[512,2048]{1,0:T(8,128)} %get-tuple-element.47, f32[2048]{0:T(1024)S(1)} %get-tuple-element.33, f32[512]{0:T(512)S(1)} %fusion.41), kind=kOutput, calls=%fused_computation.204 | convolution fusion | flops 12888047616 | bytes 41953280 | tf_op jit(solution)/shard_map/dot_general | solution.py:345
  297.8 5.8 multiply_convert_fusion.2
  305.3 11.5 %convolution_convert_fusion.2 = bf16[2048,3072]{1,0:T(8,128)(2,1)} fusion(bf16[512,2048]{1,0:T(8,128)(2,1)} %constant_dynamic-update-slice_fusion.16, bf16[512,3072]{1,0:T(8,128)(2,1)S(1)} %multiply_convert_fusion.2), kind=kOutput, calls=%fused_computation.2 | convolution fusion | flops 6448742400 | bytes 17825792 | tf_op jit(solution)/shard_map/dot_general | solution.py:51
  316.8 39.0 %all-gather.11.cloned.1.call-done = bf16[2048,3072]{1,0:T(8,128)(2,1)} async-done(((bf16[128,3072]{1,0:T(8,128)(2,1)}), bf16[2048,3072]{1,0:T(8,128)(2,1)}) %all-gather.11.cloned.1.call-update) | async-done | bytes 12582928 | tf_op jit(solution)/shard_map/all_gather | solution.py:92
  355.8 14.5 %multiply_convert_fusion.1 = (bf16[512,3072]{1,0:T(8,128)(2,1)S(1)}, bf16[512,3072]{1,0:T(8,128)(2,1)S(1)}) fusion(f32[512,6144]{1,0:T(8,128)} %fusion.45, bf16[512,2048]{1,0:T(8,128)(2,1)} %constant_dynamic-update-slice_fusion.16, bf16[2048,3072]{1,0:T(8,128)(2,1)} %all-gather.11.cloned.1.call-done), kind=kOutput, calls=%fused_computation.16 | convolution fusion | flops 6462898176 | bytes 33554432 | tf_op jit(solution)/shard_map/dot_general | solution.py:357
  370.4 19.3 %fusion.16 = bf16[512,2048]{1,0:T(8,128)(2,1)S(1)} fusion(bf16[2048,6144]{1,0:T(8,128)(2,1)} %all-gather.9.cloned.1.call-done, bf16[512,3072]{1,0:T(8,128)(2,1)S(1)} %get-tuple-element.49, bf16[512,3072]{1,0:T(8,128)(2,1)S(1)} %get-tuple-element.48), kind=kOutput, calls=%fused_computation.47 | convolution fusion | flops 12898533376 | bytes 33554432 | tf_op jit(solution)/shard_map/dot_general | solution.py:45
  391.2 20.1 %convolution_convert_fusion = bf16[2048,6144]{1,0:T(8,128)(2,1)} fusion(bf16[512,3072]{1,0:T(8,128)(2,1)} %copy-done.41, bf16[512,3072]{1,0:T(8,128)(2,1)} %copy-done.40, f32[512,2048]{1,0:T(8,128)S(1)} %copy-done.2, f32[2048]{0:T(1024)S(1)} %get-tuple-element.33, f32[512]{0:T(512)S(1)} %fusion.41), kind=kOutput, calls=%fused_computation | convolution fusion | flops 12913213440 | bytes 35661824 | tf_op jit(solution)/shard_map/dot_general | solution.py:51
  411.3 11.7 %convolution_convert_fusion.4 = bf16[512,2048]{1,0:T(8,128)(2,1)} fusion(bf16[512,3072]{1,0:T(8,128)(2,1)} %copy-done.12, bf16[2048,3072]{1,0:T(8,128)(2,1)} %all-gather.11.cloned.1.call-done), kind=kOutput, calls=%fused_computation.48 | convolution fusion | flops 6443499520 | bytes 17825792 | tf_op jit(solution)/shard_map/dot_general | solution.py:45
  423.0 14.7 %collective-permute-done.1 = bf16[512,2048]{1,0:T(8,128)(2,1)} collective-permute-done((bf16[512,2048]{1,0:T(8,128)(2,1)S(1)}, bf16[512,2048]{1,0:T(8,128)(2,1)}, u32[]{:S(2)}, u32[]{:S(2)}) %collective-permute-start.1) | collective-permute-done | bytes 2097184 | tf_op jit(solution)/shard_map/ppermute | solution.py:62
  445.3 4.5 convolution_convert_fusion.3
  449.8 4.5 convolution_convert_fusion.6
  454.4 29.8 %all_to_all.20 = bf16[4,512,256]{2,1,0:T(8,128)(2,1)} all-to-all(bf16[4,512,256]{2,1,0:T(8,128)(2,1)S(1)} %bitcast.81), channel_id=1, replica_groups=mesh['fsdp'=4,'ctx'=4,'tp'=2] {'ctx'}, dimensions={0} | all-to-all | bytes 2097152 | tf_op jit(solution)/shard_map/all_to_all | solution.py:96
  484.1 21.4 %shard_map.265 = bf16[2048,512]{1,0:T(8,128)(2,1)} custom-call(bf16[2048,512]{1,0:T(8,128)(2,1)} %bitcast.1.qkv, bf16[2048,256]{1,0:T(8,128)(2,1)} %bitcast.85, f32[2048,2]{1,0:T(8,128)} %get-tuple-element.28.lse, s32[2048,1]{1,0:T(8,128)} %copy.157.start_col, s32[1,2048]{1,0:T(1,128)} %bitcast.102, s32[2048,1]{1,0:T(8,128)} %copy.158.piece_col, ...), custom_call_target="tpu_custom_call" | custom-call | flops 9663676416 | bytes 3194880 | tf_op jit(solution)/shard_map/pallas_call | solution.py:219
  509.6 4.6 all-to-all-start.3
  526.8 41.8 %all-to-all-done.3 = bf16[4,512,512]{1,2,0:T(8,128)(2,1)} async-done(((bf16[4,512,512]{1,2,0:T(8,128)(2,1)}), bf16[4,512,512]{1,2,0:T(8,128)(2,1)}, u32[]{:S(2)}, u32[]{:S(2)}) %all-to-all-start.3) | async-done | bytes 2097184 | tf_op jit(solution)/shard_map/all_to_all | solution.py:96
  580.8 9.0 %fusion.48 = bf16[528,2048]{1,0:T(8,128)(2,1)S(1)} fusion(bf16[2048,2176]{1,0:T(8,128)(2,1)} %all-gather.5.cloned.1.call-done, bf16[512,512]{0,1:T(8,128)(2,1)S(1)} %bitcast.91, bf16[512,512]{0,1:T(8,128)(2,1)S(1)} %bitcast.93, bf16[512,1024]{0,1:T(8,128)(2,1)S(1)} %bitcast.88, bf16[528,128]{0,1:T(8,128)(2,1)S(1)} %copy-done.23), kind=kOutput, calls=%fused_computation.206 | convolution fusion | flops 4726689792 | bytes 13307904 | tf_op jit(solution)/shard_map/dot_general | solution.py:45
  596.7 12.9 %convolution_convert_fusion.1 = bf16[2048,2176]{1,0:T(8,128)(2,1)} fusion(bf16[16,2048]{1,0:T(8,128)(2,1)S(1)} %add_convert_fusion.1, bf16[512,2048]{1,0:T(8,128)(2,1)S(1)} %copy-done.17, bf16[512,512]{0,1:T(8,128)(2,1)S(1)} %bitcast.92, bf16[512,512]{0,1:T(8,128)(2,1)S(1)} %bitcast.94, bf16[512,1024]{0,1:T(8,128)(2,1)S(1)} %bitcast.89, ...), kind=kOutput, calls=%fused_computation.1 | convolution fusion | flops 4735471616 | bytes 13307904 | tf_op jit(solution)/shard_map/dot_general | solution.py:51
  613.3 46.7 %collective-permute-done.3 = bf16[512,2048]{1,0:T(8,128)(2,1)S(1)} collective-permute-done((bf16[512,2048]{1,0:T(8,128)(2,1)}, bf16[512,2048]{1,0:T(8,128)(2,1)S(1)}, u32[]{:S(2)}, u32[]{:S(2)}) %collective-permute-start.3) | collective-permute-done | bytes 2097184 | tf_op jit(solution)/shard_map/ppermute | solution.py:62
  662.8 38.4 %collective-permute-done.2 = bf16[512,2048]{1,0:T(8,128)(2,1)S(1)} collective-permute-done((bf16[512,2048]{1,0:T(8,128)(2,1)}, bf16[512,2048]{1,0:T(8,128)(2,1)S(1)}, u32[]{:S(2)}, u32[]{:S(2)}) %collective-permute-start.2) | collective-permute-done | bytes 2097184 | tf_op jit(solution)/shard_map/ppermute | solution.py:62
  701.1 6.8 fusion.12
  729.0 12.0 %reduce-scatter.11.cloned.1.call-done = bf16[128,3072]{1,0:T(8,128)(2,1)} async-done(((bf16[2048,3072]{1,0:T(8,128)(2,1)}), bf16[128,3072]{1,0:T(8,128)(2,1)}) %reduce-scatter.11.cloned.1.call-update) | async-done | bytes 786448 | tf_op jit(solution)/shard_map/reduce_scatter | solution.py:86
  743.4 136.0 %reduce-scatter.9.cloned.1.call-done = bf16[128,6144]{1,0:T(8,128)(2,1)} async-done(((bf16[2048,6144]{1,0:T(8,128)(2,1)}), bf16[128,6144]{1,0:T(8,128)(2,1)}) %reduce-scatter.9.cloned.1.call-update) | async-done | bytes 1572880 | tf_op jit(solution)/shard_map/reduce_scatter | solution.py:86
  (268 shorter events, 140.9 us)
Async XLA Ops:
  7.2 59.1 %all-gather.5.cloned.1.call-start = ((), (), s32[]{:S(2)}) async-start(), calls=%async_computation.8 | async-start | bytes 9469952 | tf_op jit(solution)/shard_map/all_gather | solution.py:92
  11.5 174.3 %all-gather.7.cloned.1.call-start = ((), (), s32[]{:S(2)}) async-start(), calls=%async_computation.9 | async-start | bytes 4456448 | tf_op jit(solution)/shard_map/all_gather | solution.py:92
  12.2 263.7 %all-gather.9.cloned.1.call-start = ((), (), s32[]{:S(2)}) async-start(), calls=%async_computation.10 | async-start | bytes 26738688 | tf_op jit(solution)/shard_map/all_gather | solution.py:92
  13.6 342.3 %all-gather.11.cloned.1.call-start = ((), (), s32[]{:S(2)}) async-start(), calls=%async_computation.11 | async-start | bytes 13369344 | tf_op jit(solution)/shard_map/all_gather | solution.py:92
  29.6 233.7 %copy-start = (bf16[512,2048]{1,0:T(8,128)(2,1)}, bf16[512,2048]{1,0:T(8,128)(2,1)S(1)}, u32[]{:S(2)}) copy-start(bf16[512,2048]{1,0:T(8,128)(2,1)S(1)} %constant_dynamic-update-slice_fusion) | copy-start | bytes 6291460
  30.1 37.3 %copy-start.35 = (f32[512]{0:T(512)}, f32[512]{0:T(512)S(1)}, u32[]{:S(2)}) copy-start(f32[512]{0:T(512)S(1)} %fusion.13) | copy-start | bytes 6148
  30.1 42.0 %copy-start.33 = (f32[512]{0:T(512)}, f32[512]{0:T(512)S(1)}, u32[]{:S(2)}) copy-start(f32[512]{0:T(512)S(1)} %fusion.40) | copy-start | bytes 6148
  30.2 41.9 %copy-start.26 = (f32[16,16]{1,0:T(8,128)}, f32[16,16]{1,0:T(8,128)S(1)}, u32[]{:S(2)}) copy-start(f32[16,16]{1,0:T(8,128)S(1)} %fusion.37) | copy-start | bytes 3076
  72.1 11.1 %copy-start.16 = (bf16[512,2048]{1,0:T(8,128)(2,1)}, bf16[512,2048]{1,0:T(8,128)(2,1)S(1)}, u32[]{:S(2)}) copy-start(bf16[512,2048]{1,0:T(8,128)(2,1)S(1)} %fusion.7) | copy-start | bytes 6291460
  89.2 65.9 %all-to-all-start = ((bf16[4,512,512]{2,1,0:T(8,128)(2,1)}), bf16[4,512,512]{2,1,0:T(8,128)(2,1)}, u32[]{:S(2)}, u32[]{:S(2)}) async-start(bf16[4,512,512]{2,1,0:T(8,128)(2,1)} %rope.1), calls=%async_computation | async-start | bytes 4194304 | tf_op jit(solution)/shard_map/all_to_all | solution.py:96
  172.0 41.4 %all-to-all-start.1 = ((bf16[4,512,256]{1,2,0:T(8,128)(2,1)}), bf16[4,512,256]{1,2,0:T(8,128)(2,1)S(1)}, u32[]{:S(2)}, u32[]{:S(2)}) async-start(bf16[4,512,256]{1,2,0:T(8,128)(2,1)} %copy.159), calls=%async_computation.1 | async-start | bytes 2097152 | tf_op jit(solution)/shard_map/all_to_all | solution.py:96
  218.4 44.9 %collective-permute-start = (bf16[512,2048]{1,0:T(8,128)(2,1)S(1)}, bf16[512,2048]{1,0:T(8,128)(2,1)S(1)}, u32[]{:S(2)}, u32[]{:S(2)}) collective-permute-start(bf16[512,2048]{1,0:T(8,128)(2,1)S(1)} %convolution_convert_fusion.5), channel_id=1, source_target_pairs={{0,1},{1,0},{2,3},{3,2},{4,5},{5,4},{6,7},{7,6},{8,9},{9,8},{10,11... | collective-permute-start | bytes 6291464 | tf_op jit(solution)/shard_map/ppermute | solution.py:62
  370.4 19.3 %copy-start.40 = (bf16[512,3072]{1,0:T(8,128)(2,1)}, bf16[512,3072]{1,0:T(8,128)(2,1)S(1)}, u32[]{:S(2)}) copy-start(bf16[512,3072]{1,0:T(8,128)(2,1)S(1)} %get-tuple-element.48) | copy-start | bytes 9437188
  370.4 19.3 %copy-start.41 = (bf16[512,3072]{1,0:T(8,128)(2,1)}, bf16[512,3072]{1,0:T(8,128)(2,1)S(1)}, u32[]{:S(2)}) copy-start(bf16[512,3072]{1,0:T(8,128)(2,1)S(1)} %get-tuple-element.49) | copy-start | bytes 9437188
  370.4 20.8 %copy-start.2 = (f32[512,2048]{1,0:T(8,128)S(1)}, f32[512,2048]{1,0:T(8,128)}, u32[]{:S(2)}) copy-start(f32[512,2048]{1,0:T(8,128)} %get-tuple-element.47) | copy-start | bytes 12582916
  389.7 48.0 %collective-permute-start.1 = (bf16[512,2048]{1,0:T(8,128)(2,1)S(1)}, bf16[512,2048]{1,0:T(8,128)(2,1)}, u32[]{:S(2)}, u32[]{:S(2)}) collective-permute-start(bf16[512,2048]{1,0:T(8,128)(2,1)S(1)} %fusion.16), channel_id=1, source_target_pairs={{0,1},{1,0},{2,3},{3,2},{4,5},{5,4},{6,7},{7,6},{8,9},{9,8},{10,11... | collective-permute-start | bytes 6291464 | tf_op jit(solution)/shard_map/ppermute | solution.py:62
  509.6 59.0 %all-to-all-start.3 = ((bf16[4,512,512]{1,2,0:T(8,128)(2,1)}), bf16[4,512,512]{1,2,0:T(8,128)(2,1)}, u32[]{:S(2)}, u32[]{:S(2)}) async-start(bf16[4,512,512]{1,2,0:T(8,128)(2,1)} %copy.163), calls=%async_computation.3 | async-start | bytes 4194304 | tf_op jit(solution)/shard_map/all_to_all | solution.py:96
  514.2 205.8 %reduce-scatter.7.cloned.1.call-start = ((), (), s32[]{:S(2)}) async-start(), calls=%async_computation.13 | async-start | bytes 4456448 | tf_op jit(solution)/shard_map/reduce_scatter | solution.py:86
  519.3 202.5 %reduce-scatter.5.cloned.1.call-start = ((), (), s32[]{:S(2)}) async-start(), calls=%async_computation.12 | async-start | bytes 9469952 | tf_op jit(solution)/shard_map/reduce_scatter | solution.py:86
  525.6 45.2 %copy-start.8 = (f32[512,4,128]{0,2,1:T(8,128)S(1)}, f32[512,4,128]{0,2,1:T(8,128)}, u32[]{:S(2)}) copy-start(f32[512,4,128]{0,2,1:T(8,128)} %copy.175) | copy-start | bytes 3145732
  580.8 9.0 %copy-start.1 = (bf16[512,2048]{1,0:T(8,128)(2,1)S(1)}, bf16[512,2048]{1,0:T(8,128)(2,1)}, u32[]{:S(2)}) copy-start(bf16[512,2048]{1,0:T(8,128)(2,1)} %copy-done) | copy-start | bytes 6291460
  580.8 9.0 %copy-start.34 = (f32[512]{0:T(512)S(1)}, f32[512]{0:T(512)}, u32[]{:S(2)}) copy-start(f32[512]{0:T(512)} %copy-done.33) | copy-start | bytes 6148
  592.3 4.3 collective-permute-start.4
  609.7 131.3 %reduce-scatter.11.cloned.1.call-start = ((), (), s32[]{:S(2)}) async-start(), calls=%async_computation.15 | async-start | bytes 13369344 | tf_op jit(solution)/shard_map/reduce_scatter | solution.py:86
  610.4 49.6 %copy-start.25 = (f32[2048]{0:T(1024)S(1)}, f32[2048]{0:T(1024)}, u32[]{:S(2)}) copy-start(f32[2048]{0:T(1024)} %copy-done.24) | copy-start | bytes 24580
  610.4 269.0 %reduce-scatter.9.cloned.1.call-start = ((), (), s32[]{:S(2)}) async-start(), calls=%async_computation.14 | async-start | bytes 26738688 | tf_op jit(solution)/shard_map/reduce_scatter | solution.py:86
  611.2 51.6 %copy-start.36 = (f32[512]{0:T(512)S(1)}, f32[512]{0:T(512)}, u32[]{:S(2)}) copy-start(f32[512]{0:T(512)} %copy-done.35) | copy-start | bytes 6148
  611.2 90.0 %copy-start.4 = (f32[512,2048]{1,0:T(8,128)S(1)}, f32[512,2048]{1,0:T(8,128)}, u32[]{:S(2)}) copy-start(f32[512,2048]{1,0:T(8,128)} %get-tuple-element.47) | copy-start | bytes 12582916
  611.2 89.9 %copy-start.6 = (bf16[512,2048]{1,0:T(8,128)(2,1)S(1)}, bf16[512,2048]{1,0:T(8,128)(2,1)}, u32[]{:S(2)}) copy-start(bf16[512,2048]{1,0:T(8,128)(2,1)} %get-tuple-element.44) | copy-start | bytes 6291460
  611.2 48.8 %collective-permute-start.3 = (bf16[512,2048]{1,0:T(8,128)(2,1)}, bf16[512,2048]{1,0:T(8,128)(2,1)S(1)}, u32[]{:S(2)}, u32[]{:S(2)}) collective-permute-start(bf16[512,2048]{1,0:T(8,128)(2,1)} %get-tuple-element.44), channel_id=1, source_target_pairs={{0,1},{1,0},{2,3},{3,2},{4,5},{5,4},{6,7},{7,6},{8,9},{9,8},{10,11... | collective-permute-start | bytes 6291464 | tf_op jit(solution)/shard_map/ppermute | solution.py:62
  612.8 88.3 %collective-permute-start.2 = (bf16[512,2048]{1,0:T(8,128)(2,1)}, bf16[512,2048]{1,0:T(8,128)(2,1)S(1)}, u32[]{:S(2)}, u32[]{:S(2)}) collective-permute-start(bf16[512,2048]{1,0:T(8,128)(2,1)} %convolution_convert_fusion.4), channel_id=1, source_target_pairs={{0,1},{1,0},{2,3},{3,2},{4,5},{5,4},{6,7},{7,6},{8,9},{9,8},{10,11... | collective-permute-start | bytes 6291464 | tf_op jit(solution)/shard_map/ppermute | solution.py:62
  708.9 11.1 %copy-start.38 = (bf16[512,2048]{1,0:T(8,128)(2,1)}, bf16[512,2048]{1,0:T(8,128)(2,1)S(1)}, u32[]{:S(2)}) copy-start(bf16[512,2048]{1,0:T(8,128)(2,1)S(1)} %constant_dynamic-update-slice_fusion.48) | copy-start | bytes 6291460
  (27 other events, 92.0 us)
Sparse Core Ops, SparseCore 0:
  11.6 54.6 all-gather.4
  67.9 47.2 all-gather.6
  117.4 158.4 all-gather.8
  277.4 78.4 all-gather.10
  519.4 75.8 reduce-scatter.6
  609.8 56.1 reduce-scatter.4
  668.2 72.6 reduce-scatter.10
  743.3 136.1 reduce-scatter.8

commit v2 on v1

--- a/solution.py
+++ b/solution.py
@@ -282,9 +282,10 @@
     for i, gain in enumerate(gains):
         side = jnp.where(side_index == i, gain[:, None], side)
     shards = width // rows
-    w_qkv = jnp.concatenate([w_query, key_weight, value_weight, side], axis=1)
-    qkv_full = gather_rows(w_qkv)
-    wo_full = gather_rows(w_out)
+    w_qkvo = jnp.concatenate([w_query, key_weight, value_weight, side, w_out], axis=1)
+    qkvo_full = gather_rows(w_qkvo)
+    qkv_full = qkvo_full[:, : qkv_cols + SIDE]
+    wo_full = qkvo_full[:, qkv_cols + SIDE :]
     gu_full = gather_rows(jnp.concatenate([w_gate, w_up], axis=1))
     wd_full = gather_rows(w_down)
     side_full = qkv_full[:, qkv_cols:]
@@ -374,7 +375,6 @@
     d_branch = d_residual.astype(bf16)
     grad_out_part = contract_first(d_branch, o_tok).astype(bf16)
     grad_out_part, d_branch = lax.optimization_barrier((grad_out_part, d_branch))
-    grad_out = scatter_sum(grad_out_part)
     d_out = (
         jnp.dot(d_branch, wo_full, preferred_element_type=f32)
         .astype(bf16)
@@ -422,9 +422,11 @@
     gain_rows = pair_sum(gain_rows)
     normed_tail = jnp.concatenate([normed_bf, gain_rows.astype(bf16)], axis=0)
     grad_qkv_part = contract_first(normed_tail, d_qkv).astype(bf16)
+    grad_qkv_part = jnp.concatenate([grad_qkv_part, grad_out_part], axis=1)
     grad_qkv_part = with_layout_constraint(grad_qkv_part, ROW_MAJOR)
     grad_qkv = scatter_sum(grad_qkv_part)
-    grad_side = grad_qkv[:, qkv_cols:]
+    grad_out = grad_qkv[:, qkv_cols + SIDE :]
+    grad_side = grad_qkv[:, qkv_cols : qkv_cols + SIDE]
     side_sums = grad_side[:, :4].astype(f32)
     return (
         layer_out,

time: 898 us -> 839 us (0.934)
  waiting for transfers between devices: 499 us -> 432 us
    reduce_scatter x4 -> x3, waiting for transfers between devices: 148 us -> 91.6 us  [scatter_sum(): lax.psum_scatter(part, BOTH, scatter_dimension=0, tiled=True, axis_index_...]
    all_gather x4 -> x3, waiting for transfers between devices: 82.7 us -> 70.8 us  [gather_rows(): lax.all_gather(shard, BOTH, axis=0, tiled=True, axis_index_groups=[ring_o...]
    unnamed x149 -> x154, local copies, waits for them, and re-layouts: 49.4 us -> 53.4 us
  transfers between devices with their start and end apart: 16 -> 14, of which waited for: 13 -> 11; matrix products, arithmetic and copies ran while one was open for 24% -> 33% of each run, Pallas kernels for 2% -> 5%
where the time goes in v2:
time: 839 us; the launch traced here: 831 us
  waiting for transfers between devices  432 us (51%)
  matrix products  146 us (17%)
  local copies, waits for them, and re-layouts  78 us (9%)
  other arithmetic  66.3 us (8%)
  Pallas kernels  42 us (5%)
  blocking collectives  29.8 us (4%)
  starting transfers between devices  20.4 us (2%)
  between operations  16.3 us (2%)
    ppermute x5, waiting for transfers between devices, pair_sum(): other = lax.ppermute(mine, 'tp', ring)  140 us
    all_to_all x3, waiting for transfers between devices, swap_ctx(): lax.all_to_all(planes, 'ctx', split_axis=0, concat_axis=0, tiled=True)  129 us
    reduce_scatter x3, waiting for transfers between devices, scatter_sum(): lax.psum_scatter(part, BOTH, scatter_dimension=0, tiled=True, axis_index_...  91.6 us
    all_gather x3, waiting for transfers between devices, gather_rows(): lax.all_gather(shard, BOTH, axis=0, tiled=True, axis_index_groups=[ring_o...  70.8 us
    unnamed x154, local copies, waits for them, and re-layouts  53.4 us
    dot_general x4, matrix products, contract_first(): lax.dot_general(left_side, right_side, (((0,), (0,)), ((), ())), preferre...  47.7 us
    dot_general x4, matrix products, contract_last(): lax.dot_general(left_side, right_side, (((1,), (1,)), ((), ())), preferre...  45.4 us
    pallas_call x2, Pallas kernels, attention_call(): pl.pallas_call(kernel, out_shape=results, in_specs=[pl.BlockSpec(memory_s...  36.1 us
  transfers between devices with their start and end apart: 14, of which 11 were waited for; matrix products, arithmetic and copies ran while one was open for 33% of the time, Pallas kernels for 5%

profile of v2, /device:TPU:0, one launch (start us, length us, event | category | flops | bytes accessed | tf_op | source)
XLA Modules:
  0.0 831.1 jit_solution(8528319542073770289)
XLA Ops:
  34.4 54.4 %all-gather.4.cloned.1.call-done = bf16[2048,3200]{1,0:T(8,128)(2,1)} async-done(((bf16[128,3200]{1,0:T(8,128)(2,1)}), bf16[2048,3200]{1,0:T(8,128)(2,1)}) %all-gather.4.cloned.1.call-update) | async-done | bytes 13107216 | tf_op jit(solution)/shard_map/all_gather | solution.py:92
  94.7 12.1 %fusion.2.raw = f32[512,2176]{1,0:T(8,128)} fusion(bf16[512,2048]{1,0:T(8,128)(2,1)S(1)} %fusion.11, bf16[2048,3200]{1,0:T(8,128)(2,1)} %all-gather.4.cloned.1.call-done), kind=kOutput, calls=%fused_computation.15 | convolution fusion | flops 4563402752 | bytes 15466496 | tf_op jit(solution)/shard_map/dot_general | solution.py:302
  106.9 5.8 rope.1
  112.7 4.9 all-to-all-start
  121.5 67.3 %all-to-all-done = bf16[4,512,512]{2,1,0:T(8,128)(2,1)} async-done(((bf16[4,512,512]{2,1,0:T(8,128)(2,1)}), bf16[4,512,512]{2,1,0:T(8,128)(2,1)}, u32[]{:S(2)}, u32[]{:S(2)}) %all-to-all-start) | async-done | bytes 2097184 | tf_op jit(solution)/shard_map/all_to_all | solution.py:96
  188.9 14.8 %shard_map.264 = (bf16[2048,256]{1,0:T(8,128)(2,1)}, f32[2048,2]{1,0:T(8,128)}) custom-call(bf16[2048,512]{1,0:T(8,128)(2,1)} %bitcast.1.qkv, s32[2048,1]{1,0:T(8,128)} %copy.157.start_col, s32[1,2048]{1,0:T(1,128)} %bitcast.97, s32[2048,1]{1,0:T(8,128)} %copy.158.piece_col, s32[1,2048]{1,0:T(1,128)} %bitcast.94), custom_call_target="tpu_custom_call" | custom-call | flops 9663676416 | bytes 2129920 | tf_op jit(solution)/shard_map/pallas_call | solution.py:219
  219.3 27.2 %all-to-all-done.1 = bf16[4,512,256]{1,2,0:T(8,128)(2,1)S(1)} async-done(((bf16[4,512,256]{1,2,0:T(8,128)(2,1)}), bf16[4,512,256]{1,2,0:T(8,128)(2,1)S(1)}, u32[]{:S(2)}, u32[]{:S(2)}) %all-to-all-start.1) | async-done | bytes 1048608 | tf_op jit(solution)/shard_map/all_to_all | solution.py:96
  246.5 5.0 fusion.25
  260.0 36.5 %collective-permute-done = bf16[512,2048]{1,0:T(8,128)(2,1)S(1)} collective-permute-done((bf16[512,2048]{1,0:T(8,128)(2,1)S(1)}, bf16[512,2048]{1,0:T(8,128)(2,1)S(1)}, u32[]{:S(2)}, u32[]{:S(2)}) %collective-permute-start) | collective-permute-done | bytes 2097184 | tf_op jit(solution)/shard_map/ppermute | solution.py:62
  299.3 22.2 %fusion.59 = f32[512,6144]{1,0:T(8,128)} fusion(bf16[2048,6144]{1,0:T(8,128)(2,1)} %all-gather.6.cloned.1.call-done, f32[512,2048]{1,0:T(8,128)} %get-tuple-element.47, f32[2048]{0:T(1024)S(1)} %get-tuple-element.33, f32[512]{0:T(512)S(1)} %fusion.55), kind=kOutput, calls=%fused_computation.217 | convolution fusion | flops 12888047616 | bytes 41953280 | tf_op jit(solution)/shard_map/dot_general | solution.py:346
  321.6 5.8 multiply_convert_fusion.2
  329.1 11.3 %convolution_convert_fusion.2 = bf16[2048,3072]{1,0:T(8,128)(2,1)} fusion(bf16[512,2048]{1,0:T(8,128)(2,1)} %constant_dynamic-update-slice_fusion.21, bf16[512,3072]{1,0:T(8,128)(2,1)S(1)} %multiply_convert_fusion.2), kind=kOutput, calls=%fused_computation.3 | convolution fusion | flops 6448742400 | bytes 17825792 | tf_op jit(solution)/shard_map/dot_general | solution.py:51
  340.5 16.4 %all-gather.8.cloned.1.call-done = bf16[2048,3072]{1,0:T(8,128)(2,1)} async-done(((bf16[128,3072]{1,0:T(8,128)(2,1)}), bf16[2048,3072]{1,0:T(8,128)(2,1)}) %all-gather.8.cloned.1.call-update) | async-done | bytes 12582928 | tf_op jit(solution)/shard_map/all_gather | solution.py:92
  356.9 14.5 %multiply_convert_fusion.1 = (bf16[512,3072]{1,0:T(8,128)(2,1)S(1)}, bf16[512,3072]{1,0:T(8,128)(2,1)S(1)}) fusion(f32[512,6144]{1,0:T(8,128)} %fusion.59, bf16[512,2048]{1,0:T(8,128)(2,1)} %constant_dynamic-update-slice_fusion.21, bf16[2048,3072]{1,0:T(8,128)(2,1)} %all-gather.8.cloned.1.call-done), kind=kOutput, calls=%fused_computation.21 | convolution fusion | flops 6462898176 | bytes 33554432 | tf_op jit(solution)/shard_map/dot_general | solution.py:358
  371.4 19.6 %fusion.24 = bf16[512,2048]{1,0:T(8,128)(2,1)S(1)} fusion(bf16[2048,6144]{1,0:T(8,128)(2,1)} %all-gather.6.cloned.1.call-done, bf16[512,3072]{1,0:T(8,128)(2,1)S(1)} %get-tuple-element.49, bf16[512,3072]{1,0:T(8,128)(2,1)S(1)} %get-tuple-element.48), kind=kOutput, calls=%fused_computation.56 | convolution fusion | flops 12898533376 | bytes 33554432 | tf_op jit(solution)/shard_map/dot_general | solution.py:45
  392.6 20.0 %convolution_convert_fusion = bf16[2048,6144]{1,0:T(8,128)(2,1)} fusion(bf16[512,3072]{1,0:T(8,128)(2,1)} %copy-done.42, bf16[512,3072]{1,0:T(8,128)(2,1)} %copy-done.41, f32[512,2048]{1,0:T(8,128)S(1)} %copy-done.2, f32[2048]{0:T(1024)S(1)} %get-tuple-element.33, f32[512]{0:T(512)S(1)} %fusion.55), kind=kOutput, calls=%fused_computation | convolution fusion | flops 12913213440 | bytes 35661824 | tf_op jit(solution)/shard_map/dot_general | solution.py:51
  412.6 11.9 %convolution_convert_fusion.4 = bf16[512,2048]{1,0:T(8,128)(2,1)} fusion(bf16[512,3072]{1,0:T(8,128)(2,1)} %copy-done.11, bf16[2048,3072]{1,0:T(8,128)(2,1)} %all-gather.8.cloned.1.call-done), kind=kOutput, calls=%fused_computation.57 | convolution fusion | flops 6443499520 | bytes 17825792 | tf_op jit(solution)/shard_map/dot_general | solution.py:45
  424.5 14.6 %collective-permute-done.1 = bf16[512,2048]{1,0:T(8,128)(2,1)} collective-permute-done((bf16[512,2048]{1,0:T(8,128)(2,1)S(1)}, bf16[512,2048]{1,0:T(8,128)(2,1)}, u32[]{:S(2)}, u32[]{:S(2)}) %collective-permute-start.1) | collective-permute-done | bytes 2097184 | tf_op jit(solution)/shard_map/ppermute | solution.py:62
  446.8 4.4 convolution_convert_fusion.3
  451.2 4.5 fusion.35
  455.8 29.8 %all_to_all.20 = bf16[4,512,256]{2,1,0:T(8,128)(2,1)} all-to-all(bf16[4,512,256]{2,1,0:T(8,128)(2,1)S(1)} %bitcast.77), channel_id=1, replica_groups=mesh['fsdp'=4,'ctx'=4,'tp'=2] {'ctx'}, dimensions={0} | all-to-all | bytes 2097152 | tf_op jit(solution)/shard_map/all_to_all | solution.py:96
  485.6 21.4 %shard_map.265 = bf16[2048,512]{1,0:T(8,128)(2,1)} custom-call(bf16[2048,512]{1,0:T(8,128)(2,1)} %bitcast.1.qkv, bf16[2048,256]{1,0:T(8,128)(2,1)} %bitcast.81, f32[2048,2]{1,0:T(8,128)} %get-tuple-element.28.lse, s32[2048,1]{1,0:T(8,128)} %copy.157.start_col, s32[1,2048]{1,0:T(1,128)} %bitcast.98, s32[2048,1]{1,0:T(8,128)} %copy.158.piece_col, ...), custom_call_target="tpu_custom_call" | custom-call | flops 9663676416 | bytes 3194880 | tf_op jit(solution)/shard_map/pallas_call | solution.py:219
  507.0 4.1 copy.163
  511.1 4.6 all-to-all-start.3
  528.9 34.1 %all-to-all-done.3 = bf16[4,512,512]{1,2,0:T(8,128)(2,1)} async-done(((bf16[4,512,512]{1,2,0:T(8,128)(2,1)}), bf16[4,512,512]{1,2,0:T(8,128)(2,1)}, u32[]{:S(2)}, u32[]{:S(2)}) %all-to-all-start.3) | async-done | bytes 2097184 | tf_op jit(solution)/shard_map/all_to_all | solution.py:96
  575.3 8.9 %fusion = bf16[528,2048]{1,0:T(8,128)(2,1)S(1)} fusion(bf16[2048,3200]{1,0:T(8,128)(2,1)} %all-gather.4.cloned.1.call-done, bf16[512,512]{0,1:T(8,128)(2,1)S(1)} %bitcast.87, bf16[512,512]{0,1:T(8,128)(2,1)S(1)} %bitcast.89, bf16[512,1024]{0,1:T(8,128)(2,1)S(1)} %bitcast.84, bf16[528,128]{0,1:T(8,128)(2,1)S(1)} %copy-done.24), kind=kOutput, calls=%fused_computation.13 | convolution fusion | flops 4726689792 | bytes 13307904 | tf_op jit(solution)/shard_map/dot_general | solution.py:45
  591.1 12.0 %convolution_convert_fusion.1 = bf16[2048,2176]{1,0:T(8,128)(2,1)S(1)} fusion(bf16[16,2048]{1,0:T(8,128)(2,1)S(1)} %add_convert_fusion.1, bf16[512,2048]{1,0:T(8,128)(2,1)S(1)} %copy-done.16, bf16[512,512]{0,1:T(8,128)(2,1)S(1)} %bitcast.88, bf16[512,512]{0,1:T(8,128)(2,1)} %bitcast.90, bf16[512,1024]{0,1:T(8,128)(2,1)S(1)} %bitcast.85, ...), kind=kOutput, calls=%fused_computation.2 | convolution fusion | flops 4735471616 | bytes 13307904 | tf_op jit(solution)/shard_map/dot_general | solution.py:51
  603.1 5.6 pad_maximum_fusion
  611.4 46.7 %collective-permute-done.3 = bf16[512,2048]{1,0:T(8,128)(2,1)S(1)} collective-permute-done((bf16[512,2048]{1,0:T(8,128)(2,1)}, bf16[512,2048]{1,0:T(8,128)(2,1)S(1)}, u32[]{:S(2)}, u32[]{:S(2)}) %collective-permute-start.3) | collective-permute-done | bytes 2097184 | tf_op jit(solution)/shard_map/ppermute | solution.py:62
  660.9 39.2 %collective-permute-done.2 = bf16[512,2048]{1,0:T(8,128)(2,1)S(1)} collective-permute-done((bf16[512,2048]{1,0:T(8,128)(2,1)}, bf16[512,2048]{1,0:T(8,128)(2,1)S(1)}, u32[]{:S(2)}, u32[]{:S(2)}) %collective-permute-start.2) | collective-permute-done | bytes 2097184 | tf_op jit(solution)/shard_map/ppermute | solution.py:62
  700.1 6.7 fusion.16
  728.9 91.6 %reduce-scatter.6.cloned.1.call-done = bf16[128,6144]{1,0:T(8,128)(2,1)} async-done(((bf16[2048,6144]{1,0:T(8,128)(2,1)}), bf16[128,6144]{1,0:T(8,128)(2,1)}) %reduce-scatter.6.cloned.1.call-update) | async-done | bytes 1572880 | tf_op jit(solution)/shard_map/reduce_scatter | solution.py:86
  (267 shorter events, 137.0 us)
Async XLA Ops:
  7.2 7.1 copy-start.21
  7.2 81.6 %all-gather.4.cloned.1.call-start = ((), (), s32[]{:S(2)}) async-start(), calls=%async_computation.7 | async-start | bytes 13926400 | tf_op jit(solution)/shard_map/all_gather | solution.py:92
  14.2 285.1 %all-gather.6.cloned.1.call-start = ((), (), s32[]{:S(2)}) async-start(), calls=%async_computation.8 | async-start | bytes 26738688 | tf_op jit(solution)/shard_map/all_gather | solution.py:92
  15.6 341.3 %all-gather.8.cloned.1.call-start = ((), (), s32[]{:S(2)}) async-start(), calls=%async_computation.9 | async-start | bytes 13369344 | tf_op jit(solution)/shard_map/all_gather | solution.py:92
  24.1 8.2 copy-start.40
  31.8 264.7 %copy-start = (bf16[512,2048]{1,0:T(8,128)(2,1)}, bf16[512,2048]{1,0:T(8,128)(2,1)S(1)}, u32[]{:S(2)}) copy-start(bf16[512,2048]{1,0:T(8,128)(2,1)S(1)} %constant_dynamic-update-slice_fusion) | copy-start | bytes 6291460
  32.3 57.6 %copy-start.36 = (f32[512]{0:T(512)}, f32[512]{0:T(512)S(1)}, u32[]{:S(2)}) copy-start(f32[512]{0:T(512)S(1)} %fusion.17) | copy-start | bytes 6148
  32.3 62.4 %copy-start.34 = (f32[512]{0:T(512)}, f32[512]{0:T(512)S(1)}, u32[]{:S(2)}) copy-start(f32[512]{0:T(512)S(1)} %fusion.54) | copy-start | bytes 6148
  32.4 62.3 %copy-start.27 = (f32[16,16]{1,0:T(8,128)}, f32[16,16]{1,0:T(8,128)S(1)}, u32[]{:S(2)}) copy-start(f32[16,16]{1,0:T(8,128)S(1)} %fusion.51) | copy-start | bytes 3076
  94.7 12.1 %copy-start.15 = (bf16[512,2048]{1,0:T(8,128)(2,1)}, bf16[512,2048]{1,0:T(8,128)(2,1)S(1)}, u32[]{:S(2)}) copy-start(bf16[512,2048]{1,0:T(8,128)(2,1)S(1)} %fusion.11) | copy-start | bytes 6291460
  112.7 76.1 %all-to-all-start = ((bf16[4,512,512]{2,1,0:T(8,128)(2,1)}), bf16[4,512,512]{2,1,0:T(8,128)(2,1)}, u32[]{:S(2)}, u32[]{:S(2)}) async-start(bf16[4,512,512]{2,1,0:T(8,128)(2,1)} %rope.1), calls=%async_computation | async-start | bytes 4194304 | tf_op jit(solution)/shard_map/all_to_all | solution.py:96
  205.9 40.6 %all-to-all-start.1 = ((bf16[4,512,256]{1,2,0:T(8,128)(2,1)}), bf16[4,512,256]{1,2,0:T(8,128)(2,1)S(1)}, u32[]{:S(2)}, u32[]{:S(2)}) async-start(bf16[4,512,256]{1,2,0:T(8,128)(2,1)} %copy.159), calls=%async_computation.1 | async-start | bytes 2097152 | tf_op jit(solution)/shard_map/all_to_all | solution.py:96
  209.4 509.5 %reduce-scatter.8.cloned.1.call-start = ((), (), s32[]{:S(2)}) async-start(), calls=%async_computation.12 | async-start | bytes 13369344 | tf_op jit(solution)/shard_map/reduce_scatter | solution.py:86
  251.5 44.9 %collective-permute-start = (bf16[512,2048]{1,0:T(8,128)(2,1)S(1)}, bf16[512,2048]{1,0:T(8,128)(2,1)S(1)}, u32[]{:S(2)}, u32[]{:S(2)}) collective-permute-start(bf16[512,2048]{1,0:T(8,128)(2,1)S(1)} %fusion.25), channel_id=1, source_target_pairs={{0,1},{1,0},{2,3},{3,2},{4,5},{5,4},{6,7},{7,6},{8,9},{9,8},{10,11... | collective-permute-start | bytes 6291464 | tf_op jit(solution)/shard_map/ppermute | solution.py:62
  371.4 19.7 %copy-start.41 = (bf16[512,3072]{1,0:T(8,128)(2,1)}, bf16[512,3072]{1,0:T(8,128)(2,1)S(1)}, u32[]{:S(2)}) copy-start(bf16[512,3072]{1,0:T(8,128)(2,1)S(1)} %get-tuple-element.48) | copy-start | bytes 9437188
  371.4 19.7 %copy-start.42 = (bf16[512,3072]{1,0:T(8,128)(2,1)}, bf16[512,3072]{1,0:T(8,128)(2,1)S(1)}, u32[]{:S(2)}) copy-start(bf16[512,3072]{1,0:T(8,128)(2,1)S(1)} %get-tuple-element.49) | copy-start | bytes 9437188
  371.4 21.2 %copy-start.2 = (f32[512,2048]{1,0:T(8,128)S(1)}, f32[512,2048]{1,0:T(8,128)}, u32[]{:S(2)}) copy-start(f32[512,2048]{1,0:T(8,128)} %get-tuple-element.47) | copy-start | bytes 12582916
  391.1 48.0 %collective-permute-start.1 = (bf16[512,2048]{1,0:T(8,128)(2,1)S(1)}, bf16[512,2048]{1,0:T(8,128)(2,1)}, u32[]{:S(2)}, u32[]{:S(2)}) collective-permute-start(bf16[512,2048]{1,0:T(8,128)(2,1)S(1)} %fusion.24), channel_id=1, source_target_pairs={{0,1},{1,0},{2,3},{3,2},{4,5},{5,4},{6,7},{7,6},{8,9},{9,8},{10,11... | collective-permute-start | bytes 6291464 | tf_op jit(solution)/shard_map/ppermute | solution.py:62
  511.1 51.9 %all-to-all-start.3 = ((bf16[4,512,512]{1,2,0:T(8,128)(2,1)}), bf16[4,512,512]{1,2,0:T(8,128)(2,1)}, u32[]{:S(2)}, u32[]{:S(2)}) async-start(bf16[4,512,512]{1,2,0:T(8,128)(2,1)} %copy.163), calls=%async_computation.3 | async-start | bytes 4194304 | tf_op jit(solution)/shard_map/all_to_all | solution.py:96
  515.7 205.6 %reduce-scatter.4.cloned.1.call-start = ((), (), s32[]{:S(2)}) async-start(), calls=%async_computation.10 | async-start | bytes 13926400 | tf_op jit(solution)/shard_map/reduce_scatter | solution.py:86
  575.3 8.9 %copy-start.1 = (bf16[512,2048]{1,0:T(8,128)(2,1)S(1)}, bf16[512,2048]{1,0:T(8,128)(2,1)}, u32[]{:S(2)}) copy-start(bf16[512,2048]{1,0:T(8,128)(2,1)} %copy-done) | copy-start | bytes 6291460
  575.3 8.9 %copy-start.35 = (f32[512]{0:T(512)S(1)}, f32[512]{0:T(512)}, u32[]{:S(2)}) copy-start(f32[512]{0:T(512)} %copy-done.34) | copy-start | bytes 6148
  586.7 4.3 collective-permute-start.4
  591.1 12.0 %copy-start.10 = (bf16[2048,1024]{1,0:T(8,128)(2,1)S(1)}, bf16[2048,1024]{1,0:T(8,128)(2,1)}, u32[]{:S(2)}) copy-start(bf16[2048,1024]{1,0:T(8,128)(2,1)} %convolution_convert_fusion.3) | copy-start | bytes 12582916
  608.7 49.4 %copy-start.26 = (f32[2048]{0:T(1024)S(1)}, f32[2048]{0:T(1024)}, u32[]{:S(2)}) copy-start(f32[2048]{0:T(1024)} %copy-done.25) | copy-start | bytes 24580
  608.7 211.7 %reduce-scatter.6.cloned.1.call-start = ((), (), s32[]{:S(2)}) async-start(), calls=%async_computation.11 | async-start | bytes 26738688 | tf_op jit(solution)/shard_map/reduce_scatter | solution.py:86
  609.3 51.6 %copy-start.37 = (f32[512]{0:T(512)S(1)}, f32[512]{0:T(512)}, u32[]{:S(2)}) copy-start(f32[512]{0:T(512)} %copy-done.36) | copy-start | bytes 6148
  609.3 90.7 %copy-start.4 = (f32[512,2048]{1,0:T(8,128)S(1)}, f32[512,2048]{1,0:T(8,128)}, u32[]{:S(2)}) copy-start(f32[512,2048]{1,0:T(8,128)} %get-tuple-element.47) | copy-start | bytes 12582916
  609.3 90.7 %copy-start.6 = (bf16[512,2048]{1,0:T(8,128)(2,1)S(1)}, bf16[512,2048]{1,0:T(8,128)(2,1)}, u32[]{:S(2)}) copy-start(bf16[512,2048]{1,0:T(8,128)(2,1)} %get-tuple-element.44) | copy-start | bytes 6291460
  609.4 48.8 %collective-permute-start.3 = (bf16[512,2048]{1,0:T(8,128)(2,1)}, bf16[512,2048]{1,0:T(8,128)(2,1)S(1)}, u32[]{:S(2)}, u32[]{:S(2)}) collective-permute-start(bf16[512,2048]{1,0:T(8,128)(2,1)} %get-tuple-element.44), channel_id=1, source_target_pairs={{0,1},{1,0},{2,3},{3,2},{4,5},{5,4},{6,7},{7,6},{8,9},{9,8},{10,11... | collective-permute-start | bytes 6291464 | tf_op jit(solution)/shard_map/ppermute | solution.py:62
  610.9 89.2 %collective-permute-start.2 = (bf16[512,2048]{1,0:T(8,128)(2,1)}, bf16[512,2048]{1,0:T(8,128)(2,1)S(1)}, u32[]{:S(2)}, u32[]{:S(2)}) collective-permute-start(bf16[512,2048]{1,0:T(8,128)(2,1)} %convolution_convert_fusion.4), channel_id=1, source_target_pairs={{0,1},{1,0},{2,3},{3,2},{4,5},{5,4},{6,7},{7,6},{8,9},{9,8},{10,11... | collective-permute-start | bytes 6291464 | tf_op jit(solution)/shard_map/ppermute | solution.py:62
  707.7 11.1 %copy-start.39 = (bf16[512,2048]{1,0:T(8,128)(2,1)}, bf16[512,2048]{1,0:T(8,128)(2,1)S(1)}, u32[]{:S(2)}) copy-start(bf16[512,2048]{1,0:T(8,128)(2,1)S(1)} %constant_dynamic-update-slice_fusion.53) | copy-start | bytes 6291460
  (26 other events, 89.4 us)
Sparse Core Ops, SparseCore 0:
  14.3 74.4 all-gather.3
  91.0 185.6 all-gather.5
  278.3 78.5 all-gather.7
  359.1 72.4 reduce-scatter.7
  608.9 73.2 reduce-scatter.3
  684.3 136.1 reduce-scatter.5
